TPU v7x, 32 devices: a whole 2x2x4 slice. The times are simulated.
32 devices in a mesh: section: 2 (over core), seq: 4 (over z), head: 4 (over y, x).
Axes of the slice: x: 2, y: 2, z: 4, core: 2. Of those that a mesh axis runs over, the one named last changes fastest.
Arguments:
- inputs: bfloat16 [2, 1024, 1536], P(None, 'seq'), may hold values from -6 to 6
- segments: int32 [2, 1024], P(None, 'seq'), may hold values from 0 to 31, never falling along the last dimension, each value on 1 to 768 neighbouring positions
- norms: float32 [2, 2, 1536], P('section'), may hold values from 0.25 to 1.75
- rec_in: bfloat16 [1536, 2, 2048], P(None, None, 'head'), may hold values from -0.15625 to 0.15625
- rec_gates: bfloat16 [16, 128, 2, 128], P('head'), may hold values from -0.5 to 0.5
- rec_chan: float32 [8, 2048], P(None, 'head'), may hold values from -20 to 4
- rec_out: bfloat16 [2048, 1536], P('head'), may hold values from -0.125 to 0.125
- attn_q: bfloat16 [1536, 1536], P(None, 'head'), may hold values from -0.15625 to 0.15625
- attn_kv: bfloat16 [1536, 256], replicated, may hold values from -0.15625 to 0.15625
- attn_out: bfloat16 [1536, 1536], P('head'), may hold values from -0.4375 to 0.4375
- mlp_in: bfloat16 [2, 1536, 2, 4608], P('section', None, None, 'head'), may hold values from -0.15625 to 0.15625
- mlp_out: bfloat16 [2, 4608, 1536], P('section', 'head'), may hold values from -0.09375 to 0.09375
- cotangent: bfloat16 [2, 1024, 1536], P(None, 'seq'), may hold values from -6 to 6
Outputs:
- final_out: bfloat16 [2, 1024, 1536], P('section', 'seq')
- grad_inputs: float32 [2, 1024, 1536], P('section', 'seq')
- grad_norms: float32 [2, 2, 1536], P('section', None, 'seq')
- grad_rec_in: float32 [1536, 2, 2048], P(('section', 'seq'), None, 'head')
- grad_rec_gates: float32 [16, 128, 2, 128], P('head', ('section', 'seq'))
- grad_rec_chan: float32 [8, 2048], P('section', 'head')
- grad_rec_out: float32 [2048, 1536], P('head', ('section', 'seq'))
- grad_attn_q: float32 [1536, 1536], P(('section', 'seq'), 'head')
- grad_attn_kv: float32 [1536, 256], P(('section', 'seq'))
- grad_attn_out: float32 [1536, 1536], P('head', ('section', 'seq'))
- grad_mlp_in: float32 [2, 1536, 2, 4608], P('section', 'seq', None, 'head')
- grad_mlp_out: float32 [2, 4608, 1536], P('section', 'head', 'seq')
Inputs may be any that keep to these rules, and one draw needn't show every extreme that they name: `segments`: along each stream segment numbers never fall and rise by one at each new document; a document holds 1 to 768 tokens, and one in every stream holds exactly 768.
All inputs are finite; a program needn't handle non-finite values.
Results may differ from a plain program's by a relative error of at most 0.03.
Values may be sent and summed in bfloat16 or wider, within the bound.
A program may use at most 320 MiB of HBM per device.

v0:
```python
import functools

import jax
import jax.numpy as jnp
from jax import lax
from jax.experimental import pallas as pl
from jax.experimental.pallas import tpu as pltpu
from jax.sharding import PartitionSpec as P

WINDOW = 1024
EPSILON = 1e-06
MESH = pl.DeviceIdType.MESH
F32 = jnp.float32
BF16 = jnp.bfloat16
SWAP = [(0, 1), (1, 0)]


def dot(a, b, dims, out=F32):
    return lax.dot_general(a, b, ((dims[:1], dims[1:]), ((), ())), preferred_element_type=F32).astype(
        out
    )


def vmem():
    return pl.BlockSpec(memory_space=pltpu.VMEM)


def meet(axis, me, n):
    barrier = pltpu.get_barrier_semaphore()
    for k in range(1, n):
        peer = lax.rem(me + k, n)
        pl.semaphore_signal(barrier, inc=1, device_id={axis: peer}, device_id_type=MESH)
    pl.semaphore_wait(barrier, n - 1)


def remote(src, dst, send, recv, axis, peer):
    return pltpu.make_async_remote_copy(
        src_ref=src,
        dst_ref=dst,
        send_sem=send,
        recv_sem=recv,
        device_id={axis: peer},
        device_id_type=MESH,
    )


def scatter_start(n, me, rows, part, recv, send_sem, recv_sem):
    copies = []
    for k in range(1, n):
        peer = lax.rem(me + k, n)
        start = pl.multiple_of(peer * rows, rows)
        copies.append(
            remote(
                part.at[pl.ds(start, rows)],
                recv.at[k - 1],
                send_sem.at[k - 1],
                recv_sem.at[k - 1],
                "head",
                peer,
            )
        )
    for copy in copies:
        copy.start()
    return copies


def scatter_sum(me, rows, part, recv, copies):
    total = part[pl.ds(pl.multiple_of(me * rows, rows), rows)].astype(F32)
    for k, copy in enumerate(copies):
        copy.wait_recv()
        total = total + recv[k].astype(F32)
    return total


def drain(copies):
    for copy in copies:
        copy.wait_send()


def spread(n, me, rows, value, full, send_sem, recv_sem):
    mine = pl.ds(pl.multiple_of(me * rows, rows), rows)
    full[mine] = value
    copies = []
    for k in range(1, n):
        peer = lax.rem(me + k, n)
        copies.append(
            remote(
                full.at[mine], full.at[mine], send_sem.at[k - 1], recv_sem.at[k - 1], "head", peer
            )
        )
    for copy in copies:
        copy.start()
    return copies


def finish(copies):
    for copy in copies:
        copy.wait()


def forward_body(n, kind, part, base, gain, new, full, recv, s1, r1, s2, r2):
    me = lax.axis_index("head")
    rows = base.shape[0]
    meet("head", me, n)
    sent = scatter_start(n, me, rows, part, recv, s1, r1)
    fresh = base[...] + scatter_sum(me, rows, part, recv, sent)
    new[...] = fresh
    out = fresh
    if kind != "last":
        out = fresh * lax.rsqrt(jnp.mean(fresh * fresh, axis=-1, keepdims=True) + EPSILON)
        out = out * gain[...]
    finish(spread(n, me, rows, out.astype(BF16), full, s2, r2))
    drain(sent)


def forward_mlp_body(n, part, base, gain, own_in, own_out, other_in, other_out, *refs):
    new, full, gate_up, hidden, part_next, recv, s1, r1, s2, r2, acc, b_in, b_out, sems = refs
    own, other = (own_in, own_out), (other_in, other_out)
    fetch_weights(0, own, other, (b_in, b_out), sems)
    forward_body(n, "keep", part, base, gain, new, full, recv, s1, r1, s2, r2)
    wait_weights(own, (b_in, b_out), sems)
    mlp_forward_part(full, (b_in, b_out), gate_up, hidden, part_next, acc)


def forward_both_body(n, part, base, gain, low, own_in, own_out, other_in, other_out, *refs):
    new, full, hidden, mine, theirs, part_last, part_back = refs[:7]
    recv, s1, r1, s2, r2, acc, acc_back, b_in, b_out, sems = refs[7:]
    own, other = (own_in, own_out), (other_in, other_out)
    fetch_weights(1, own, other, (b_in, b_out), sems)
    forward_body(n, "keep", part, base, gain, new, full, recv, s1, r1, s2, r2)
    wait_weights(own, (b_in, b_out), sems)
    mlp_both_part(
        full, low, (b_in, b_out), hidden, mine, theirs, part_last, part_back, acc, acc_back
    )


def meet_around(n, me, blocks, place, pairs):
    barrier = pltpu.get_barrier_semaphore()
    for d, k in pairs:
        device = {
            "seq": lax.rem(place - d + blocks, blocks),
            "head": lax.rem(me - k + n, n),
        }
        pl.semaphore_signal(barrier, inc=1, device_id=device, device_id_type=MESH)
    pl.semaphore_wait(barrier, len(pairs))


def keys_body(n, blocks, reach, part, base, gain, w_kv, new, full, keys, recv, s1, r1, s2, r2, own, s3, r3):
    me, place = lax.axis_index("head"), lax.axis_index("seq")
    rows = base.shape[0]
    count = part.shape[0]
    pairs = [(d, k) for d in range(reach + 1) for k in range(n) if (d, k) != (0, 0)]
    meet_around(n, me, blocks, place, pairs)
    sent = scatter_start(n, me, rows, part, recv, s1, r1)
    fresh = base[...] + scatter_sum(me, rows, part, recv, sent)
    fresh = fresh.astype(BF16).astype(F32)
    new[...] = fresh
    out = fresh * lax.rsqrt(jnp.mean(fresh * fresh, axis=-1, keepdims=True) + EPSILON)
    low = (out * gain[...]).astype(BF16)
    value = jnp.dot(low, w_kv[...], preferred_element_type=F32).astype(BF16)
    own[...] = value
    mine = pl.multiple_of(me * rows, rows)
    keys[pl.ds(reach * count + mine, rows)] = value
    copies = []
    for d, k in pairs:
        copies.append(
            pltpu.make_async_remote_copy(
                src_ref=own,
                dst_ref=keys.at[pl.ds((reach - d) * count + mine, rows)],
                send_sem=s3.at[d * n + k],
                recv_sem=r3.at[d * n + k],
                device_id={
                    "seq": lax.rem(place + d, blocks),
                    "head": lax.rem(me + k, n),
                },
                device_id_type=MESH,
            )
        )
    for copy in copies:
        copy.start()
    finish(spread(n, me, rows, low, full, s2, r2))
    finish(copies)
    drain(sent)


def norm_back_rows(grad, v, gain, up):
    scale = lax.rsqrt(jnp.mean(v * v, axis=-1, keepdims=True) + EPSILON)
    gain_grad = jnp.sum(grad * v * scale, axis=0, keepdims=True)
    inner = grad * gain
    out = up + scale * inner - v * (
        scale * scale * scale * jnp.mean(inner * v, axis=-1, keepdims=True)
    )
    return out, gain_grad


def backward_body(n, part, base, gain, up, res, gain_grad, full, recv, s1, r1, s2, r2):
    me = lax.axis_index("head")
    rows = base.shape[0]
    meet("head", me, n)
    sent = scatter_start(n, me, rows, part, recv, s1, r1)
    grad = scatter_sum(me, rows, part, recv, sent)
    out, gain_grad[...] = norm_back_rows(grad, base[...], gain[...], up[...])
    res[...] = out
    finish(spread(n, me, rows, out.astype(BF16), full, s2, r2))
    drain(sent)


def keys_back_body(
    n, blocks, reach, part, base, gain, up, grad_kv, w_kv, gate_up, own_in, own_out, other_in, other_out,
    res, gain_grad, full, kv_full, mine_out, theirs_out, part_next,
    recv, s1, r1, s2, r2, recv_kv, s3, r3, send_z, recv_z, s4, r4, s5, r5, acc, b_in, b_out, sems,
):
    own, other = (own_in, own_out), (other_in, other_out)
    fetch_weights(0, own, other, (b_in, b_out), sems)
    me, place = lax.axis_index("head"), lax.axis_index("seq")
    rows = base.shape[0]
    meet_around(
        n,
        me,
        blocks,
        place,
        [(0, k) for k in range(1, n)] + [(-d, 0) for d in range(1, reach + 1)],
    )
    mine = pl.ds(pl.multiple_of(me * rows, rows), rows)
    kv_sent = []
    for k in range(1, n):
        peer = lax.rem(me + k, n)
        there = pl.ds(pl.multiple_of(peer * rows, rows), rows)
        kv_sent.append(
            remote(
                grad_kv.at[:, there], recv_kv.at[k - 1], s3.at[k - 1], r3.at[k - 1], "head", peer
            )
        )
    for copy in kv_sent:
        copy.start()
    sent = scatter_start(n, me, rows, part, recv, s1, r1)
    total = grad_kv[:, mine].astype(F32)
    for k, copy in enumerate(kv_sent):
        copy.wait_recv()
        total = total + recv_kv[k].astype(F32)
    send_z[...] = total.astype(BF16)
    z_sent = []
    for d in range(1, reach + 1):
        z_sent.append(
            remote(
                send_z.at[reach - d],
                recv_z.at[d - 1],
                s4.at[d - 1],
                r4.at[d - 1],
                "seq",
                lax.rem(place - d + blocks, blocks),
            )
        )
    for copy in z_sent:
        copy.start()
    grad = scatter_sum(me, rows, part, recv, sent)
    own_kv = total[reach]
    for d, copy in enumerate(z_sent):
        copy.wait_recv()
        own_kv = own_kv + recv_z[d].astype(F32)
    kv_low = own_kv.astype(BF16)
    kv_spread = spread(n, me, rows, kv_low, kv_full, s5, r5)
    grad = grad + lax.dot_general(
        kv_low, w_kv[...], (((1,), (1,)), ((), ())), preferred_element_type=F32
    )
    out, gain_grad[...] = norm_back_rows(grad, base[...], gain[...], up[...])
    low = out.astype(BF16)
    res[...] = low.astype(F32)
    finish(spread(n, me, rows, low, full, s2, r2))
    finish(kv_spread)
    drain(sent + kv_sent + z_sent)
    wait_weights(own, (b_in, b_out), sems)
    mlp_backward_part(full, gate_up, (b_in, b_out), mine_out, theirs_out, part_next, acc)


def boundary_scratch(n, rows, width):
    return [pltpu.VMEM((n - 1, rows, width), BF16)] + [pltpu.SemaphoreType.DMA((n - 1,))] * 4


def join_forward(kind, part, base, gain, ident):
    n = lax.axis_size("head")
    count, width = part.shape
    rows = base.shape[0]
    return pl.pallas_call(
        functools.partial(forward_body, n, kind),
        out_shape=(
            jax.ShapeDtypeStruct((rows, width), F32),
            jax.ShapeDtypeStruct((count, width), BF16),
        ),
        in_specs=[vmem()] * 3,
        out_specs=(vmem(), vmem()),
        scratch_shapes=boundary_scratch(n, rows, width),
        compiler_params=pltpu.CompilerParams(collective_id=ident, has_side_effects=True),
    )(part, base, gain)


def join_mlp(part, base, gain, weights, ident, low=None):
    n = lax.axis_size("head")
    count, width = part.shape
    rows = base.shape[0]
    units = weights[1].shape[0]
    whole = jax.ShapeDtypeStruct((count, width), BF16)
    narrow = jax.ShapeDtypeStruct((count, units), BF16)
    outs = [jax.ShapeDtypeStruct((rows, width), F32), whole]
    if low is None:
        body, operands = forward_mlp_body, [part, base, gain]
        outs += [jax.ShapeDtypeStruct((TILES, count, 2 * units // TILES), F32), narrow, whole]
    else:
        body, operands = forward_both_body, [part, base, gain, low]
        outs += [narrow, narrow, narrow, whole, whole]
    return pl.pallas_call(
        functools.partial(body, n),
        out_shape=tuple(outs),
        in_specs=[vmem()] * len(operands) + [pl.BlockSpec(memory_space=pl.ANY)] * 4,
        out_specs=tuple(vmem() for _ in outs),
        scratch_shapes=boundary_scratch(n, rows, width)
        + mlp_scratch(count, width, units, 1 if low is None else 2),
        compiler_params=pltpu.CompilerParams(collective_id=ident, has_side_effects=True),
    )(*operands, *weights)


def join_keys(part, base, gain, w_kv, reach, ident):
    n, blocks = lax.axis_size("head"), lax.axis_size("seq")
    count, width = part.shape
    rows = base.shape[0]
    both = w_kv.shape[1]
    slots = (reach + 1) * n
    return pl.pallas_call(
        functools.partial(keys_body, n, blocks, reach),
        name="join_keys",
        out_shape=(
            jax.ShapeDtypeStruct((rows, width), F32),
            jax.ShapeDtypeStruct((count, width), BF16),
            jax.ShapeDtypeStruct(((reach + 1) * count, both), BF16),
        ),
        in_specs=[vmem()] * 4,
        out_specs=(vmem(), vmem(), vmem()),
        scratch_shapes=boundary_scratch(n, rows, width)
        + [
            pltpu.VMEM((rows, both), BF16),
            pltpu.SemaphoreType.DMA((slots,)),
            pltpu.SemaphoreType.DMA((slots,)),
        ],
        compiler_params=pltpu.CompilerParams(collective_id=ident, has_side_effects=True),
    )(part, base, gain, w_kv)


def join_backward(part, base, gain, up, ident):
    n = lax.axis_size("head")
    count, width = part.shape
    rows = base.shape[0]
    return pl.pallas_call(
        functools.partial(backward_body, n),
        out_shape=(
            jax.ShapeDtypeStruct((rows, width), F32),
            jax.ShapeDtypeStruct((1, width), F32),
            jax.ShapeDtypeStruct((count, width), BF16),
        ),
        in_specs=[vmem()] * 4,
        out_specs=(vmem(), vmem(), vmem()),
        scratch_shapes=boundary_scratch(n, rows, width),
        compiler_params=pltpu.CompilerParams(collective_id=ident, has_side_effects=True),
    )(part, base, gain, up)


def join_keys_back(part, base, gain, up, grad_kv, w_kv, gate_up, weights, ident):
    n, blocks = lax.axis_size("head"), lax.axis_size("seq")
    count, width = part.shape
    rows = base.shape[0]
    reach, both = grad_kv.shape[0] - 1, grad_kv.shape[2]
    units = weights[1].shape[0]
    dma = pltpu.SemaphoreType.DMA
    return pl.pallas_call(
        functools.partial(keys_back_body, n, blocks, reach),
        name="join_keys_back",
        out_shape=(
            jax.ShapeDtypeStruct((rows, width), F32),
            jax.ShapeDtypeStruct((1, width), F32),
            jax.ShapeDtypeStruct((count, width), BF16),
            jax.ShapeDtypeStruct((count, both), BF16),
            jax.ShapeDtypeStruct((count, units), BF16),
            jax.ShapeDtypeStruct((count, units), BF16),
            jax.ShapeDtypeStruct((count, width), BF16),
        ),
        in_specs=[vmem()] * 7 + [pl.BlockSpec(memory_space=pl.ANY)] * 4,
        out_specs=tuple([vmem()] * 7),
        scratch_shapes=boundary_scratch(n, rows, width)
        + [
            pltpu.VMEM((n - 1, reach + 1, rows, both), BF16),
            dma((n - 1,)),
            dma((n - 1,)),
            pltpu.VMEM((reach + 1, rows, both), BF16),
            pltpu.VMEM((reach, rows, both), BF16),
            dma((reach,)),
            dma((reach,)),
            dma((n - 1,)),
            dma((n - 1,)),
        ]
        + mlp_scratch(count, width, units, 1),
        compiler_params=pltpu.CompilerParams(collective_id=ident, has_side_effects=True),
    )(part, base, gain, up, grad_kv, w_kv, gate_up, *weights)


def totals_body(heads, blocks, gains, chan, gates, gain_out, chan_out, gate_out, *scratch):
    g1, g2, g3, sum_one, sum_two, c2, c3, csum, w2, sems = scratch
    head, place, core = lax.axis_index("head"), lax.axis_index("seq"), lax.axis_index("section")
    barrier = pltpu.get_barrier_semaphore()
    for axis, me, n in (("head", head, heads), ("seq", place, blocks), ("section", core, 2)):
        for k in range(1, n):
            pl.semaphore_signal(
                barrier, inc=1, device_id={axis: lax.rem(me + k, n)}, device_id_type=MESH
            )
    pl.semaphore_wait(barrier, heads + blocks - 1)
    used = 0

    def exchange(src, slots, axis, me, n, split=False):
        nonlocal used
        copies = []
        for k in range(1, n):
            peer = lax.rem(me + k, n)
            copies.append(
                remote(
                    src.at[peer] if split else src,
                    slots.at[k - 1],
                    sems.at[0, used],
                    sems.at[1, used],
                    axis,
                    peer,
                )
            )
            used += 1
        for copy in copies:
            copy.start()
        return copies

    def collect(copies, src, slots):
        total = src[...]
        for k, copy in enumerate(copies):
            copy.wait_recv()
            total = total + slots[k]
        return total

    by_head = exchange(gains, g1, "head", head, heads)
    chan_seq = exchange(chan, c2, "seq", place, blocks)
    gate_seq = exchange(gates, w2, "seq", place, blocks, True)
    sum_one[...] = collect(by_head, gains, g1)
    gain_seq = exchange(sum_one, g2, "seq", place, blocks)
    csum[...] = collect(chan_seq, chan, c2)
    chan_core = exchange(csum, c3, "section", core, 2)
    sum_two[...] = collect(gain_seq, sum_one, g2)
    gain_core = exchange(sum_two, g3, "section", core, 2)
    chan_out[...] = collect(chan_core, csum, c3)
    gain_out[...] = collect(gain_core, sum_two, g3)
    gate_total = gates[place].astype(F32)
    for k, copy in enumerate(gate_seq):
        copy.wait_recv()
        gate_total = gate_total + w2[k].astype(F32)
    gate_out[...] = gate_total.astype(BF16)
    for copy in by_head + chan_seq + gate_seq + gain_seq + chan_core + gain_core:
        copy.wait_send()


def totals(gains, chan, gates, ident):
    heads, blocks = lax.axis_size("head"), lax.axis_size("seq")
    gs, cs, ws = gains.shape, chan.shape, gates.shape[1:]
    return pl.pallas_call(
        functools.partial(totals_body, heads, blocks),
        name="totals",
        out_shape=(
            jax.ShapeDtypeStruct(gs, F32),
            jax.ShapeDtypeStruct(cs, F32),
            jax.ShapeDtypeStruct(ws, BF16),
        ),
        in_specs=[vmem(), vmem(), vmem()],
        out_specs=(vmem(), vmem(), vmem()),
        scratch_shapes=[
            pltpu.VMEM((heads - 1,) + gs, F32),
            pltpu.VMEM((blocks - 1,) + gs, F32),
            pltpu.VMEM((1,) + gs, F32),
            pltpu.VMEM(gs, F32),
            pltpu.VMEM(gs, F32),
            pltpu.VMEM((blocks - 1,) + cs, F32),
            pltpu.VMEM((1,) + cs, F32),
            pltpu.VMEM(cs, F32),
            pltpu.VMEM((blocks - 1,) + ws, BF16),
            pltpu.SemaphoreType.DMA((2, heads + 3 * blocks)),
        ],
        compiler_params=pltpu.CompilerParams(collective_id=ident, has_side_effects=True),
    )(gains, chan, gates)


OVER_LAST = (((1,), (1,)), ((), ()))
TILES = 3


def weight_copies(own, buffers, sems):
    tile = buffers[1].shape[1]
    copies = []
    for t in range(TILES):
        units = pl.ds(t * tile, tile)
        for k in range(2):
            copies.append(
                pltpu.make_async_copy(
                    own[0].at[k, :, units],
                    buffers[0].at[t, :, pl.ds(k * tile, tile)],
                    sems.at[k, t],
                )
            )
        copies.append(pltpu.make_async_copy(own[1].at[units], buffers[1].at[t], sems.at[2, t]))
    return copies


def fetch_weights(layer, own, other, buffers, sems):
    core = lax.axis_index("section")
    for near, use in ((own, core == layer), (other, core != layer)):

        @pl.when(use)
        def _(near=near):
            for copy in weight_copies(near, buffers, sems):
                copy.start()


def wait_weights(own, buffers, sems):
    for copy in weight_copies(own, buffers, sems):
        copy.wait()


def tile_columns(t, tile):
    return pl.ds(pl.multiple_of(t * tile, 128), tile)


def grad_tile(low, gate, up, w_in, w_out, mine, theirs, columns_at, acc):
    grad_hidden = lax.dot_general(low, w_out, OVER_LAST, preferred_element_type=F32)
    act, slope = gelu_parts(gate)
    grad_gate = (grad_hidden * up * slope).astype(BF16)
    grad_up = (grad_hidden * act).astype(BF16)
    swap = lax.axis_index("section") == 0
    mine[:, columns_at] = jnp.where(swap, grad_gate, grad_up)
    theirs[:, columns_at] = jnp.where(swap, grad_up, grad_gate)
    both = jnp.concatenate([grad_gate, grad_up], axis=1)
    acc[...] += lax.dot_general(both, w_in, OVER_LAST, preferred_element_type=F32)
    return act


def mlp_forward_part(x, buffers, gate_up, hidden, part, acc):
    tile = buffers[1].shape[1]
    acc[...] = jnp.zeros_like(acc)

    @pl.loop(0, TILES)
    def _(t):
        both = jnp.dot(x[...], buffers[0][t], preferred_element_type=F32)
        gate_up[t] = both
        low = (gelu_parts(both[:, :tile])[0] * both[:, tile:]).astype(BF16)
        hidden[:, tile_columns(t, tile)] = low
        acc[...] += jnp.dot(low, buffers[1][t], preferred_element_type=F32)

    part[...] = acc[...].astype(BF16)


def mlp_backward_part(low, gate_up, buffers, mine, theirs, part, acc):
    tile = buffers[1].shape[1]
    acc[...] = jnp.zeros_like(acc)

    @pl.loop(0, TILES)
    def _(t):
        grad_tile(
            low[...], gate_up[t, :, :tile], gate_up[t, :, tile:], buffers[0][t], buffers[1][t],
            mine, theirs, tile_columns(t, tile), acc,
        )

    part[...] = acc[...].astype(BF16)


def mlp_both_part(x, low, buffers, hidden, mine, theirs, part, part_back, acc, acc_back):
    tile = buffers[1].shape[1]
    acc[...] = jnp.zeros_like(acc)
    acc_back[...] = jnp.zeros_like(acc_back)

    @pl.loop(0, TILES)
    def _(t):
        both = jnp.dot(x[...], buffers[0][t], preferred_element_type=F32)
        gate, up = both[:, :tile], both[:, tile:]
        at = tile_columns(t, tile)
        act = grad_tile(low[...], gate, up, buffers[0][t], buffers[1][t], mine, theirs, at, acc_back)
        value = (act * up).astype(BF16)
        hidden[:, at] = value
        acc[...] += jnp.dot(value, buffers[1][t], preferred_element_type=F32)

    part[...] = acc[...].astype(BF16)
    part_back[...] = acc_back[...].astype(BF16)


def mlp_scratch(count, width, units, accs):
    tile = units // TILES
    return [pltpu.VMEM((count, width), F32)] * accs + [
        pltpu.VMEM((TILES, width, 2 * tile), BF16),
        pltpu.VMEM((TILES, tile, width), BF16),
        pltpu.SemaphoreType.DMA((3, TILES)),
    ]


def weight_grad_body(sizes, core, *refs):
    out = refs[-1]
    over = (((0,), (0,)), ((), ()))
    start = 0
    for t, size in enumerate(sizes):
        left, left_other, right, right_other = refs[4 * t : 4 * t + 4]
        spare = right.shape[1] - size
        if spare:
            window = pl.ds(pl.multiple_of(core[0] * spare, 128), size)
            near, far = right[:, window], right_other[:, window]
        else:
            near, far = right[...], right_other[...]
        total = lax.dot_general(left[...], near, over, preferred_element_type=F32)
        total += lax.dot_general(left_other[...], far, over, preferred_element_type=F32)
        out[:, start : start + size] = total.astype(BF16)
        start += size


def weight_grad(core, terms, half):
    count, width = terms[0][0].shape
    tile = 256
    steps = width // tile // (2 if half else 1)
    sizes = [term[4] for term in terms]
    in_specs, operands = [], []
    for left, left_other, right, right_other, _ in terms:
        if half:
            rows = pl.BlockSpec((count, tile), lambda i, core: (0, core[0] * steps + i))
        else:
            rows = pl.BlockSpec((count, tile), lambda i, core: (0, i))
        full = pl.BlockSpec(right.shape, lambda i, core: (0, 0))
        in_specs += [rows, rows, full, full]
        operands += [left, left_other, right, right_other]
    return pl.pallas_call(
        functools.partial(weight_grad_body, sizes),
        grid_spec=pltpu.PrefetchScalarGridSpec(
            num_scalar_prefetch=1,
            grid=(steps,),
            in_specs=in_specs,
            out_specs=pl.BlockSpec((tile, sum(sizes)), lambda i, core: (i, 0)),
        ),
        out_shape=jax.ShapeDtypeStruct((steps * tile, sum(sizes)), BF16),
    )(core, *operands)


def carry_body(n, reverse, edge, *refs):
    me = lax.axis_index("seq")
    if reverse:
        out, every, send_sem, recv_sem = refs
    else:
        ids, out, all_ids, every, send_sem, recv_sem, send_ids, recv_ids = refs
        all_ids[me] = ids[...]
    meet("seq", me, n)
    copies = []
    for k in range(1, n):
        peer = lax.rem(me + k, n)
        copies.append(
            remote(edge, every.at[k - 1], send_sem.at[k - 1], recv_sem.at[k - 1], "seq", peer)
        )
        if not reverse:
            copies.append(
                remote(ids, all_ids.at[me], send_ids.at[k - 1], recv_ids.at[k - 1], "seq", peer)
            )
    for copy in copies:
        copy.start()
    finish(copies)
    state = jnp.zeros((1, edge.shape[1]), F32)
    order = range(1, n) if reverse else range(n - 1, 0, -1)
    for k in order:
        sender = me - k if not reverse else me + n - k
        inside = sender >= 0 if not reverse else sender < n
        if reverse:
            inside = jnp.logical_and(inside, sender > me)
        slot = every[k - 1]
        state = jnp.where(inside, slot[0:1] * state + slot[1:2], state)
    out[...] = jnp.broadcast_to(state, out.shape)


def carry(edge, ident, ids=None):
    n = lax.axis_size("seq")
    dma = pltpu.SemaphoreType.DMA((n - 1,))
    scratch = [pltpu.VMEM((n - 1,) + edge.shape, F32), dma, dma]
    shapes = [jax.ShapeDtypeStruct(edge.shape, F32)]
    operands = [edge]
    if ids is not None:
        scratch += [dma, dma]
        shapes.append(jax.ShapeDtypeStruct((n,) + ids.shape, jnp.int32))
        operands.append(ids)
    return pl.pallas_call(
        functools.partial(carry_body, n, ids is None),
        out_shape=tuple(shapes),
        in_specs=[vmem() for _ in operands],
        out_specs=tuple(vmem() for _ in shapes),
        scratch_shapes=scratch,
        compiler_params=pltpu.CompilerParams(collective_id=ident, has_side_effects=True),
    )(*operands)


def shifted(x, by, row, fill):
    count = x.shape[0]
    if by > 0:
        return jnp.where(row >= by, pltpu.roll(x, by, 0), fill)
    return jnp.where(row < count + by, pltpu.roll(x, count + by, 0), fill)


def scan_rows(a, b, row, sign):
    step = 1
    while step < a.shape[0]:
        b = b + a * shifted(b, sign * step, row, 0.0)
        a = a * shifted(a, sign * step, row, 1.0)
        step *= 2
    return a, b


def minus_expm1(y):
    series = jnp.full_like(y, 1.0)
    for k in range(9, 1, -1):
        series = 1.0 + y * series * (1.0 / k)
    return jnp.where(y > -0.5, -y * series, 1.0 - jnp.exp(y))


def gelu_parts(x):
    c = 0.7978845608028654
    inner = c * (x + 0.044715 * x * x * x)
    t = jnp.tanh(inner)
    act = 0.5 * x * (1.0 + t)
    slope = 0.5 * (1.0 + t) + 0.5 * x * (1.0 - t * t) * c * (1.0 + 3.0 * 0.044715 * x * x)
    return act, slope


def same_rows(ids, k):
    return (pltpu.roll(ids, k, 0)[16:] == ids[16:]).astype(F32)


def rec_forward_body(
    x, gain, w_in, ids, chan, soft, gates,
    normed, gate_pre, ext, conv_out, pre_out, through, local, edge, low_x,
):
    count, block = conv_out.shape

    @pl.when(pl.program_id(0) == 0)
    def _():
        v = x[...].astype(F32)
        out = v * lax.rsqrt(jnp.mean(v * v, axis=-1, keepdims=True) + EPSILON) * gain[...]
        low = out.astype(BF16)
        low_x[...] = low
        normed[...] = low[16:]

    values = jnp.dot(low_x[...], w_in[0], preferred_element_type=F32).astype(BF16)
    gate_pre[...] = jnp.dot(low_x[16:], w_in[1], preferred_element_type=F32)
    ext[...] = values
    wide = values.astype(F32)
    total = chan[4:5] + chan[0:1] * wide[16:]
    for k in range(1, 4):
        total = total + chan[k : k + 1] * pltpu.roll(wide, k, 0)[16:] * same_rows(ids[...], k)
    low = total.astype(BF16)
    conv_out[...] = low
    pre = jnp.dot(low, gates[0], preferred_element_type=F32)
    rate = pre[:, :block] + chan[5:6]
    gate = pre[:, block:] + chan[6:7]
    pre_out[0] = rate
    pre_out[1] = gate
    log_decay = -8.0 * jax.nn.sigmoid(rate) * soft[...]
    decay = jnp.exp(log_decay) * same_rows(ids[...], 1)
    drive = jnp.sqrt(minus_expm1(2.0 * log_decay)) * jax.nn.sigmoid(gate) * low.astype(F32)
    row = lax.broadcasted_iota(jnp.int32, (count, block), 0)
    a, b = scan_rows(decay, drive, row, 1)
    through[...] = a
    local[...] = b
    edge[0:1] = a[count - 1 :]
    edge[1:2] = b[count - 1 :]
    edge[2:8] = jnp.zeros((6, block), F32)


def rec_forward(x, gain, w_in, ids, chan, soft, gates):
    count, width = x.shape[0] - 16, x.shape[1]
    chans = w_in.shape[2]
    blocks, block = gates.shape[:2]
    wide = pl.BlockSpec((count, block), lambda i: (0, i))
    row8 = pl.BlockSpec((8, block), lambda i: (0, i))
    tall = pl.BlockSpec((count + 16, block), lambda i: (0, i))
    f32 = jax.ShapeDtypeStruct((count, chans), F32)
    return pl.pallas_call(
        rec_forward_body,
        name="rec_forward",
        grid=(blocks,),
        out_shape=(
            jax.ShapeDtypeStruct((count, width), BF16),
            f32,
            jax.ShapeDtypeStruct((count + 16, chans), BF16),
            jax.ShapeDtypeStruct((count, chans), BF16),
            jax.ShapeDtypeStruct((2, count, chans), F32),
            f32,
            f32,
            jax.ShapeDtypeStruct((8, chans), F32),
        ),
        in_specs=[
            pl.BlockSpec((count + 16, width), lambda i: (0, 0)),
            pl.BlockSpec((1, width), lambda i: (0, 0)),
            pl.BlockSpec((2, width, block), lambda i: (0, 0, i)),
            pl.BlockSpec((count + 16, 128), lambda i: (0, 0)),
            row8,
            pl.BlockSpec((1, block), lambda i: (0, i)),
            pl.BlockSpec((1, block, 2 * block), lambda i: (i, 0, 0)),
        ],
        out_specs=(
            pl.BlockSpec((count, width), lambda i: (0, 0)),
            wide,
            tall,
            wide,
            pl.BlockSpec((2, count, block), lambda i: (0, 0, i)),
            wide,
            wide,
            row8,
        ),
        scratch_shapes=[pltpu.VMEM((count + 16, width), BF16)],
    )(x, gain, w_in, ids, chan, soft, gates)


def rec_finish_body(steps, local, through, entering, gate_pre, w_out, hidden, mixed, part, acc):
    step = pl.program_id(0)

    @pl.when(step == 0)
    def _():
        acc[...] = jnp.zeros_like(acc)

    state = local[...] + through[...] * entering[0:1]
    hidden[...] = state
    low = (state * gelu_parts(gate_pre[...])[0]).astype(BF16)
    mixed[...] = low
    acc[...] += jnp.dot(low, w_out[...], preferred_element_type=F32)

    @pl.when(step == steps - 1)
    def _():
        part[...] = acc[...].astype(BF16)


def rec_finish(local, through, entering, gate_pre, w_out):
    count, chans = local.shape
    width = w_out.shape[1]
    tile = chans // 2
    wide = pl.BlockSpec((count, tile), lambda i: (0, i))
    return pl.pallas_call(
        functools.partial(rec_finish_body, 2),
        name="rec_finish",
        grid=(2,),
        out_shape=(
            jax.ShapeDtypeStruct((count, chans), F32),
            jax.ShapeDtypeStruct((count, chans), BF16),
            jax.ShapeDtypeStruct((count, width), BF16),
        ),
        in_specs=[
            wide,
            wide,
            pl.BlockSpec((8, tile), lambda i: (0, i)),
            wide,
            pl.BlockSpec((tile, width), lambda i: (i, 0)),
        ],
        out_specs=(wide, wide, pl.BlockSpec((count, width), lambda i: (0, 0))),
        scratch_shapes=[pltpu.VMEM((count, width), F32)],
    )(local, through, entering, gate_pre, w_out)


def rec_back_first_body(gm, gate_pre, hidden, rate, soft, ids, grad_gate, beyond, local, edge):
    count, block = gm.shape
    act, slope = gelu_parts(gate_pre[...])
    up = gm[...]
    grad_gate[...] = (up * hidden[...] * slope).astype(BF16)
    decay = jnp.exp(-8.0 * jax.nn.sigmoid(rate[0]) * soft[...]) * same_rows(ids[...], 1)
    row = lax.broadcasted_iota(jnp.int32, (count, block), 0)
    a, b = scan_rows(shifted(decay, -1, row, 1.0), up * act, row, -1)
    beyond[...] = a
    local[...] = b
    edge[0:1] = decay[0:1] * a[0:1]
    edge[1:2] = decay[0:1] * b[0:1]
    edge[2:8] = jnp.zeros((6, block), F32)


def rec_back_first(gm, gate_pre, hidden, pre, soft, ids, block):
    count, chans = gm.shape
    wide = pl.BlockSpec((count, block), lambda i: (0, i))
    row8 = pl.BlockSpec((8, block), lambda i: (0, i))
    return pl.pallas_call(
        rec_back_first_body,
        name="rec_back_first",
        grid=(chans // block,),
        out_shape=(
            jax.ShapeDtypeStruct((count, chans), BF16),
            jax.ShapeDtypeStruct((count, chans), F32),
            jax.ShapeDtypeStruct((count, chans), F32),
            jax.ShapeDtypeStruct((8, chans), F32),
        ),
        in_specs=[
            wide,
            wide,
            wide,
            pl.BlockSpec((1, count, block), lambda i: (0, 0, i)),
            pl.BlockSpec((1, block), lambda i: (0, i)),
            pl.BlockSpec((count + 16, 128), lambda i: (0, 0)),
        ],
        out_specs=(wide, wide, wide, row8),
    )(gm, gate_pre, hidden, pre, soft, ids)


def rec_back_second_body(
    core, beyond, local, arriving, hidden, entering, pre, conv, chan, soft, gates, ids, ext,
    mine, theirs, grad_values, edge, chan_grad,
):
    count, block = local.shape
    row = lax.broadcasted_iota(jnp.int32, (count, block), 0)
    state = local[...] + beyond[...] * arriving[0:1]
    earlier = jnp.where(row >= 1, pltpu.roll(hidden[...], 1, 0), entering[0:1])
    low = conv[...].astype(F32)
    keep_rate = jax.nn.sigmoid(pre[0])
    log_decay = -8.0 * keep_rate * soft[...]
    decay = jnp.exp(log_decay)
    size = jnp.sqrt(minus_expm1(2.0 * log_decay))
    gate = jax.nn.sigmoid(pre[1])
    grad_decay = state * earlier * same_rows(ids[...], 1)
    grad_log = grad_decay * decay - state * gate * low * (decay * decay / size)
    grad_rate = grad_log * (-8.0 * soft[...]) * keep_rate * (1.0 - keep_rate)
    grad_gate = state * size * low * gate * (1.0 - gate)
    rate_low = grad_rate.astype(BF16)
    gate_low_part = grad_gate.astype(BF16)
    swap = core[0] == 0
    mine[...] = jnp.where(swap, rate_low, gate_low_part)
    theirs[...] = jnp.where(swap, gate_low_part, rate_low)
    weights = gates[0]
    over = (((1,), (1,)), ((), ()))
    grad_conv = (
        state * size * gate
        + lax.dot_general(rate_low, weights[:, :block], over, preferred_element_type=F32)
        + lax.dot_general(gate_low_part, weights[:, block:], over, preferred_element_type=F32)
    )
    wide = ext[...].astype(F32)
    total = chan[0:1] * grad_conv
    chan_grad[0:1] = jnp.sum(grad_conv * wide[16:], axis=0, keepdims=True)
    row8 = lax.broadcasted_iota(jnp.int32, (8, block), 0)
    over_edge = jnp.zeros((8, block), F32)
    for k in range(1, 4):
        masked = grad_conv * same_rows(ids[...], k)
        chan_grad[k : k + 1] = jnp.sum(masked * pltpu.roll(wide, k, 0)[16:], axis=0, keepdims=True)
        back = chan[k : k + 1] * masked
        total = total + shifted(back, -k, row, 0.0)
        first = back[0:8]
        if k < 3:
            first = pltpu.roll(first, 3 - k, 0)
        over_edge = over_edge + jnp.where((row8 >= 3 - k) & (row8 < 3), first, 0.0)
    grad_values[...] = total
    edge[...] = over_edge
    chan_grad[4:5] = jnp.sum(grad_conv, axis=0, keepdims=True)
    chan_grad[5:6] = jnp.sum(grad_rate, axis=0, keepdims=True)
    chan_grad[6:7] = jnp.sum(grad_gate, axis=0, keepdims=True)
    chan_grad[7:8] = jnp.sum(grad_log * keep_rate, axis=0, keepdims=True) * (
        -8.0 * jax.nn.sigmoid(chan[7:8])
    )


def rec_back_second(core, beyond, local, arriving, hidden, entering, pre, conv, chan, soft, gates, ids, ext):
    count, chans = local.shape
    blocks, block = gates.shape[:2]
    wide = pl.BlockSpec((count, block), lambda i, core: (0, i))
    row8 = pl.BlockSpec((8, block), lambda i, core: (0, i))
    pair = pl.BlockSpec((2, count, block), lambda i, core: (0, 0, i))
    low = jax.ShapeDtypeStruct((count, chans), BF16)
    return pl.pallas_call(
        rec_back_second_body,
        name="rec_back_second",
        grid_spec=pltpu.PrefetchScalarGridSpec(
            num_scalar_prefetch=1,
            grid=(blocks,),
            in_specs=[
                wide,
                wide,
                row8,
                wide,
                row8,
                pair,
                wide,
                row8,
                pl.BlockSpec((1, block), lambda i, core: (0, i)),
                pl.BlockSpec((1, block, 2 * block), lambda i, core: (i, 0, 0)),
                pl.BlockSpec((count + 16, 128), lambda i, core: (0, 0)),
                pl.BlockSpec((count + 16, block), lambda i, core: (0, i)),
            ],
            out_specs=(wide, wide, wide, row8, row8),
        ),
        out_shape=(
            low,
            low,
            jax.ShapeDtypeStruct((count, chans), F32),
            jax.ShapeDtypeStruct((8, chans), F32),
            jax.ShapeDtypeStruct((8, chans), F32),
        ),
    )(core, beyond, local, arriving, hidden, entering, pre, conv, chan, soft, gates, ids, ext)


def from_behind(array, axis, by):
    devices = lax.axis_size(axis)
    pairs = [(i, i + by) for i in range(devices) if 0 <= i + by < devices]
    return lax.ppermute(array, axis, pairs)


def swapped(array):
    return lax.ppermute(array, "section", SWAP)


def attend(query_rows, key_rows, allowed):
    head_dim = query_rows.shape[2]
    scores = jnp.einsum(
        "qhd,kd->hqk", query_rows, key_rows[:, :head_dim], preferred_element_type=F32
    ) * head_dim ** (-0.5)
    masked = jnp.where(allowed[None], scores, -1e30)
    row_max = jnp.max(masked, axis=-1, keepdims=True)
    lifted = jnp.exp(masked - row_max)
    row_total = jnp.sum(lifted, axis=-1, keepdims=True)
    weights = (lifted / row_total).astype(BF16)
    attended = jnp.einsum(
        "hqk,kd->qhd", weights, key_rows[:, head_dim:], preferred_element_type=F32
    ).astype(BF16)
    return (attended, row_max[:, :, 0] + jnp.log(row_total[:, :, 0]))


def attend_back(query_rows, key_rows, allowed, log_total, grad_rows):
    head_dim = query_rows.shape[2]
    factor = head_dim ** (-0.5)
    scores = (
        jnp.einsum("qhd,kd->hqk", query_rows, key_rows[:, :head_dim], preferred_element_type=F32)
        * factor
    )
    probs = jnp.exp(jnp.where(allowed[None], scores, -1e30) - log_total[:, :, None])
    weights = probs.astype(BF16)
    grad_probs = jnp.einsum(
        "qhd,kd->hqk", grad_rows, key_rows[:, head_dim:], preferred_element_type=F32
    )
    grad_values = jnp.einsum("hqk,qhd->kd", weights, grad_rows, preferred_element_type=F32)
    grad_scores = (
        probs * (grad_probs - jnp.sum(grad_probs * probs, axis=-1, keepdims=True))
    ).astype(BF16)
    grad_query = (
        jnp.einsum("hqk,kd->qhd", grad_scores, key_rows[:, :head_dim], preferred_element_type=F32)
        * factor
    )
    grad_keys = (
        jnp.einsum("hqk,qhd->kd", grad_scores, query_rows, preferred_element_type=F32) * factor
    )
    return (grad_query, jnp.concatenate([grad_keys, grad_values], axis=-1))


def seq_scatter(grad):
    return lax.psum_scatter(grad, "seq", scatter_dimension=0, tiled=True)


def on_device(
    inputs,
    segments,
    norms,
    rec_in,
    rec_gates,
    rec_chan,
    rec_out,
    attn_q,
    attn_kv,
    attn_out,
    mlp_in,
    mlp_out,
    cotangent,
):
    core = lax.axis_index("section")
    first = core == 0
    place = lax.axis_index("seq")
    rank = lax.axis_index("head")
    heads = lax.axis_size("head")
    blocks_seq = lax.axis_size("seq")
    _, count, width = inputs.shape
    rows = count // heads
    chans = rec_in.shape[2]
    blocks, block = rec_gates.shape[:2]

    def pick(array, index):
        return lax.dynamic_index_in_dim(array, index, 0, keepdims=False)

    def own_rows(array):
        return lax.dynamic_slice_in_dim(array, rank * rows, rows, axis=0)

    core_ref = core[None].astype(jnp.int32)
    ids = pick(segments, core)
    stream_low = pick(inputs, core)
    top_low = pick(cotangent, core)
    before = from_behind(stream_low[-16:], "seq", 1)
    reach = min(max(1, WINDOW // count), blocks_seq - 1)
    before_ids = from_behind(ids, "seq", 1)

    own_in = jnp.swapaxes(mlp_in[0], 0, 1)
    own_out = mlp_out[0]
    other_in, other_out, other_norms = swapped(own_in), swapped(own_out), swapped(norms[0])
    gains = [
        jnp.where(first, norms[0], other_norms),
        jnp.where(first, other_norms, norms[0]),
    ]
    gain = [[gains[l][k][None] for k in range(2)] for l in range(2)]
    weights = (own_in, own_out, other_in, other_out)
    rec_in_wide = jnp.swapaxes(rec_in, 0, 1)

    before_ids = jnp.where(place == 0, -1, before_ids[-16:])
    ext_ids = jnp.broadcast_to(jnp.concatenate([before_ids, ids])[:, None], (count + 16, 128))
    soft = jax.nn.softplus(rec_chan[7:8])
    gates_flat = rec_gates.reshape(blocks, block, 2 * block)
    normed_one, gate_pre, ext, conv_low, pre, through, local, edge = rec_forward(
        jnp.concatenate([before, stream_low]),
        gain[0][0],
        rec_in_wide,
        ext_ids,
        rec_chan,
        soft,
        gates_flat,
    )
    entering, every_id = carry(edge, 0, ids[None])
    hidden_state, mixed, part = rec_finish(local, through, entering, gate_pre, rec_out)
    stream_rows = own_rows(stream_low).astype(F32)
    res_one, normed_a, gate_up_a, hidden_a, part = join_mlp(
        part, stream_rows, gain[0][1], weights, 1
    )
    passed, normed_two, all_keys = join_keys(part, res_one, gain[1][0], attn_kv, reach, 2)

    head_dim = attn_kv.shape[1] // 2
    heads_here = attn_q.shape[1] // head_dim
    queries = dot(normed_two, attn_q, (1, 0), BF16).reshape(count, heads_here, head_dim)
    key_ids = jnp.concatenate(
        [
            pick(every_id, lax.rem(place - distance + blocks_seq, blocks_seq))[0]
            for distance in range(reach, 0, -1)
        ]
        + [ids]
    )
    key_spots = (place - reach) * count + jnp.arange((reach + 1) * count, dtype=jnp.int32)
    query_spots = place * count + jnp.arange(count, dtype=jnp.int32)
    distance_q = query_spots[:, None] - key_spots[None, :]
    inside = (distance_q >= 0) & (distance_q < WINDOW) & (key_spots >= 0)[None, :]
    allowed = inside & (ids[:, None] == key_ids[None, :])
    attended, log_totals = attend(queries, all_keys, allowed)
    attended = attended.reshape(count, heads_here * head_dim)
    part = dot(attended, attn_out, (1, 0), BF16)
    res_two, normed_b, hidden_b, mine_b, theirs_b, part_last, part_b = join_mlp(
        part, passed, gain[1][1], weights, 3, top_low
    )

    units = hidden_b.shape[1]
    window = (units // 2 + 127) // 128 * 128

    def mlp_term(mine, theirs, normed, hidden, out_low, out_other):
        return [
            (normed, swapped(normed), mine, swapped(theirs), units),
            (out_low, out_other, hidden, swapped(hidden), window),
        ]

    terms = mlp_term(mine_b, theirs_b, normed_b, hidden_b, top_low, pick(cotangent, 1 - core))
    part, sum_b = lax.optimization_barrier((part_b, weight_grad(core_ref, terms, False)))
    sum_b = seq_scatter(sum_b)
    grad_res_two, gain_b, low_two = join_backward(
        part, res_two, gain[1][1], own_rows(top_low).astype(F32), 5
    )

    grad_att = dot(low_two, attn_out, (1, 1), BF16)
    grad_query, grad_kv = attend_back(
        queries, all_keys, allowed, log_totals, grad_att.reshape(count, heads_here, head_dim)
    )
    query_low = grad_query.reshape(count, heads_here * head_dim).astype(BF16)
    part = dot(query_low, attn_q, (1, 1), BF16)
    grad_passed, gain_two, low_passed, kv_low, mine_a, theirs_a, part = join_keys_back(
        part,
        passed,
        gain[1][0],
        grad_res_two,
        grad_kv.astype(BF16).reshape(reach + 1, count, 2 * head_dim),
        attn_kv,
        gate_up_a,
        weights,
        6,
    )

    normed_two_other = swapped(normed_two)
    width_q, width_kv = query_low.shape[1], kv_low.shape[1]
    attn_terms = [
        (normed_two, normed_two_other, query_low, swapped(query_low), width_q),
        (normed_two, normed_two_other, kv_low, swapped(kv_low), width_kv),
        (low_two, swapped(low_two), attended, swapped(attended), width_q),
    ]
    terms = mlp_term(mine_a, theirs_a, normed_a, hidden_a, low_passed, swapped(low_passed))
    part, sum_a = lax.optimization_barrier((part, weight_grad(core_ref, terms, False)))
    sum_a = seq_scatter(sum_a)
    grad_res_one, gain_a, mix_low = join_backward(part, res_one, gain[0][1], grad_passed, 7)

    grad_mixed = dot(mix_low, rec_out, (1, 1))
    grad_branch, beyond, local_grad, edge = rec_back_first(
        grad_mixed, gate_pre, hidden_state, pre, soft, ext_ids, block
    )
    (arriving,) = carry(edge, 9)
    gate_mine, gate_theirs, grad_values, over_edge, chan_grad = rec_back_second(
        core_ref, beyond, local_grad, arriving, hidden_state, entering, pre, conv_low, rec_chan,
        soft, gates_flat, ext_ids, ext,
    )
    from_next = from_behind(over_edge[:3], "seq", -1)
    grad_values = jnp.concatenate([grad_values[:-3], grad_values[-3:] + from_next]).astype(BF16)
    part = (
        dot(grad_values, rec_in_wide[0], (1, 1)) + dot(grad_branch, rec_in_wide[1], (1, 1))
    ).astype(BF16)
    normed_one_other = swapped(normed_one)
    rec_sum = weight_grad(
        core_ref,
        [
            (normed_one, normed_one_other, grad_values, swapped(grad_values), chans),
            (normed_one, normed_one_other, grad_branch, swapped(grad_branch), chans),
            (mix_low, swapped(mix_low), mixed, swapped(mixed), chans),
        ]
        + attn_terms,
        True,
    )
    part, rec_sum = lax.optimization_barrier((part, rec_sum))
    rec_sum = seq_scatter(rec_sum)
    _, gain_one, grad_inputs = join_backward(part, stream_rows, gain[0][0], grad_res_one, 8)

    def gate_grad(left, right):
        return jnp.einsum(
            "tnb,tnc->bnc",
            left.reshape(count, blocks, block),
            right.reshape(count, blocks, block),
            preferred_element_type=F32,
        )

    gate_sum = gate_grad(conv_low, gate_mine) + gate_grad(swapped(conv_low), swapped(gate_theirs))
    share = block // (2 * blocks_seq)
    gate_sum = jnp.swapaxes(
        gate_sum.astype(BF16).reshape(2, blocks_seq, share, chans), 0, 1
    ).reshape(blocks_seq, 2 * share, chans)
    gain_rows = jnp.concatenate([gain_one, gain_a, gain_two, gain_b], axis=0)
    gain_total, chan_total, gate_sum = totals(gain_rows, chan_grad, gate_sum, 11)
    gate_sum = gate_sum.reshape(2, share, chans)
    share_norm = width // blocks_seq
    grad_norms = lax.dynamic_slice_in_dim(
        pick(gain_total.reshape(2, 2, width), core), place * share_norm, share_norm, axis=1
    )
    grad_chan = jnp.where(first, chan_total[:4], chan_total[4:])

    own_part = jnp.where(first, sum_a, sum_b)
    other_part = swapped(jnp.where(first, sum_b, sum_a))
    lower = jnp.where(first, own_part, other_part).astype(F32)
    upper = jnp.where(first, other_part, own_part).astype(F32)
    grad_mlp_in = jnp.stack([lower[:, :units], upper[:, :units]], axis=1)
    grad_mlp_out = jnp.concatenate(
        [lower[:, units:].T, upper[:, 2 * window :].T], axis=0
    )
    part_last, grad_mlp_in, grad_mlp_out, grad_norms = lax.optimization_barrier(
        (part_last, grad_mlp_in, grad_mlp_out, grad_norms)
    )
    _, final = join_forward("last", part_last, res_two, gain[1][1], 4)

    chans_q = attn_q.shape[1]
    rec_sum = rec_sum.astype(F32)
    attn_sum = rec_sum[:, 3 * chans :]
    grad_q = attn_sum[:, :chans_q]
    grad_kv_out = attn_sum[:, chans_q : chans_q + 2 * head_dim]
    grad_attn_out = attn_sum[:, chans_q + 2 * head_dim :].T
    grad_in = rec_sum[:, : 2 * chans].reshape(-1, 2, chans)
    grad_rec_out = rec_sum[:, 2 * chans : 3 * chans].T
    own_gate = pick(gate_sum, core)
    other_gate = swapped(pick(gate_sum, 1 - core))
    grad_gates = jnp.transpose(
        jnp.stack([jnp.where(first, own_gate, other_gate), jnp.where(first, other_gate, own_gate)])
        .astype(F32)
        .reshape(2, share, blocks, block),
        (2, 1, 0, 3),
    )
    return (
        final[None],
        grad_inputs.astype(F32)[None],
        grad_norms[None],
        grad_in,
        grad_gates,
        grad_chan,
        grad_rec_out,
        grad_q,
        grad_kv_out,
        grad_attn_out,
        grad_mlp_in[None],
        grad_mlp_out[None],
    )


def solution(mesh):
    in_specs = (
        P(None, "seq", None),
        P(None, "seq"),
        P("section", None, None),
        P(None, None, "head"),
        P("head", None, None, None),
        P(None, "head"),
        P("head", None),
        P(None, "head"),
        P(),
        P("head", None),
        P("section", None, None, "head"),
        P("section", "head", None),
        P(None, "seq", None),
    )
    out_specs = (
        P("section", "seq", None),
        P("section", "seq", None),
        P("section", None, "seq"),
        P(("section", "seq"), None, "head"),
        P("head", ("section", "seq"), None, None),
        P("section", "head"),
        P("head", ("section", "seq")),
        P(("section", "seq"), "head"),
        P(("section", "seq"), None),
        P("head", ("section", "seq")),
        P("section", "seq", None, "head"),
        P("section", "head", "seq"),
    )

    return jax.shard_map(
        on_device, mesh=mesh, in_specs=in_specs, out_specs=out_specs, check_vma=False
    )
```

profile of v0, /device:TPU:0, one launch (start us, length us, event | category | flops | bytes accessed | tf_op | source)
XLA Modules:
  0.0 503.1 jit_solution(17207333414323739271)
XLA Ops:
  7.3 6.9 %copy.99 = bf16[1,1536,2,1152]{3,1,2,0:T(8,128)(2,1)} copy(bf16[1,1536,2,1152]{3,2,1,0:T(2,128)(2,1)} %param.23) | data formatting | bytes 14155776 | tf_op args[10]
  14.6 5.1 %collective-permute-start.2 = (s32[256]{0:T(256)S(1)}, s32[256]{0:T(256)}, u32[]{:S(2)}, u32[]{:S(2)}) collective-permute-start(s32[256]{0:T(256)S(1)} %bitcast.201), channel_id=1, source_target_pairs={{0,4},{4,8},{8,12},{1,5},{5,9},{9,13},{2,6},{6,10},{10,14},{3,7},{... | collective-permute-start | bytes 3080 | tf_op jit(solution)/shard_map/ppermute | solution.py:1001
  19.7 1.4 dynamic-slice_bitcast_fusion.3
  21.1 3.5 collective-permute-start
  28.8 1.9 bitcast_convert_fusion.1
  32.0 4.1 copy.100
  39.8 1.7 pad_maximum_fusion.2.x
  42.3 8.1 %rec_forward.1 = (bf16[256,1536]{1,0:T(8,128)(2,1)}, f32[256,512]{1,0:T(8,128)}, bf16[272,512]{1,0:T(8,128)(2,1)}, bf16[256,512]{1,0:T(8,128)(2,1)}, f32[2,256,5...) custom-call(bf16[272,1536]{1,0:T(8,128)(2,1)} %pad_maximum_fusion.2.x, ...), custom_call_target="tpu_custom_call" | custom-call | tf_op jit(solution)/shard_map/rec_forward/pallas_call | solution.py:783
  50.4 7.1 %shard_map.220 = (f32[8,512]{1,0:T(8,128)}, s32[4,1,256]{2,1,0:T(1,128)}) custom-call(f32[8,512]{1,0:T(8,128)} %get-tuple-element.80.edge, s32[1,256]{1,0:T(1,128)} %copy-done.40), custom_call_target="tpu_custom_call" | custom-call | tf_op jit(solution)/shard_map/pallas_call | solution.py:689
  57.5 3.5 rec_finish.1
  62.0 28.0 %shard_map.221 = (f32[64,1536]{1,0:T(8,128)}, bf16[256,1536]{1,0:T(8,128)(2,1)}, f32[3,256,768]{2,1,0:T(8,128)}, bf16[256,1152]{1,0:T(8,128)(2,1)}, bf16[256,1536]{1,0:T(8,128)(2,1)}) custom-call(bf16[256,1536]{1,0:T(8,128)(2,1)} %get-tuple-element.83.part, f32[64,1536]{1,0:T(8,128)} %get-tuple-element.190.base, f32[1,1536]{1,0:T(1,128)} %get-tuple-element.178.gain, ...), custom_call_target="tpu_custom_call" | custom-call | tf_op jit(solution)/shard_map/pallas_call | solution.py:311
  90.1 32.4 %join_keys.1 = (f32[64,1536]{1,0:T(8,128)}, bf16[256,1536]{1,0:T(8,128)(2,1)}, bf16[1024,256]{1,0:T(8,128)(2,1)}) custom-call(bf16[256,1536]{1,0:T(8,128)(2,1)} %get-tuple-element.84.part, f32[64,1536]{1,0:T(8,128)} %get-tuple-element.85.base, f32[1,1536]{1,0:T(1,128)} %get-tuple-element.177.gain, bf16[1536,256]{1,0:T(8,128)(2,1)} %w_kv.3), custom_call_target="tpu_custom_call" | custom-call | tf_op jit(solution)/shard_map/join_keys/pallas_call | solution.py:328
  122.5 1.7 convolution_convert_fusion.3
  124.3 1.7 fusion.7
  129.2 1.5 convolution_convert_fusion.1.part
  130.6 33.5 %shard_map.222 = (f32[64,1536]{1,0:T(8,128)}, bf16[256,1536]{1,0:T(8,128)(2,1)}, bf16[256,1152]{1,0:T(8,128)(2,1)}, bf16[256,1152]{1,0:T(8,128)(2,1)}, bf16[256,...) custom-call(bf16[256,1536]{1,0:T(8,128)(2,1)} %convolution_convert_fusion.1.part, ...), custom_call_target="tpu_custom_call" | custom-call | tf_op jit(solution)/shard_map/pallas_call | solution.py:311
  164.8 2.8 collective-permute-done.6.refs_3_
  170.1 8.9 %shard_map.223 = bf16[1536,1792]{1,0:T(8,128)(2,1)} custom-call(s32[1]{0:T(128)} %bitcast.22.core, bf16[256,1536]{1,0:T(8,128)(2,1)} %get-tuple-element.92.refs_0_, bf16[256,1536]{1,0:T(8,128)(2,1)} %copy-done.24, bf16[256,1152]{1,0:T(8,128)(2,1)} %get-tuple-element.93.refs_2_, bf16[256,1152]{1,0:T(8,128)(2,1)} %copy-done.27, ...), custom_call_target="tpu_custom_call" | custom-call | tf_op jit(solution)/shard_map/pallas_call | solution.py:634
  180.2 2.6 fusion.1
  182.8 25.9 %shard_map.224 = (f32[64,1536]{1,0:T(8,128)}, f32[1,1536]{1,0:T(1,128)}, bf16[256,1536]{1,0:T(8,128)(2,1)}) custom-call(bf16[256,1536]{1,0:T(8,128)(2,1)} %get-tuple-element.96.part, f32[64,1536]{1,0:T(8,128)} %get-tuple-element.97.base, f32[1,1536]{1,0:T(1,128)} %get-tuple-element.176.gain, f32[64,1536]{1,0:T(8,128)} %get-tuple-element.189.up), custom_call_target="tpu_custom_call" | custom-call | tf_op jit(solution)/shard_map/pallas_call | solution.py:352
  208.7 1.7 convolution_convert_fusion.2
  210.6 3.2 fusion.2
  217.2 1.5 convolution_convert_fusion.part
  218.7 38.0 %join_keys_back.1 = (f32[64,1536]{1,0:T(8,128)}, f32[1,1536]{1,0:T(1,128)}, bf16[256,1536]{1,0:T(8,128)(2,1)}, bf16[256,256]{1,0:T(8,128)(2,1)}, bf16[256,1152]{...) custom-call(bf16[256,1536]{1,0:T(8,128)(2,1)} %convolution_convert_fusion.part, ...), custom_call_target="tpu_custom_call" | custom-call | tf_op jit(solution)/shard_map/join_keys_back/pallas_call | solution.py:373
  257.4 2.7 collective-permute-done.11.refs_7_
  262.0 8.7 %shard_map.225 = bf16[1536,1792]{1,0:T(8,128)(2,1)} custom-call(s32[1]{0:T(128)} %bitcast.22.core, bf16[256,1536]{1,0:T(8,128)(2,1)} %get-tuple-element.102.refs_0_, bf16[256,1536]{1,0:T(8,128)(2,1)} %collective-permute-done.8.refs_1_, bf16[256,1152]{1,0:T(8,128)(2,1)} %get-tuple-element.103.refs_2_, bf16[256,1152]{1,0:T(8,128)(2,1)} %copy-done.28, ...), custom_call_target="tpu_custom_call" | custom-call | tf_op jit(solution)/shard_map/pallas_call | solution.py:634
  274.6 26.0 %shard_map.226 = (f32[64,1536]{1,0:T(8,128)}, f32[1,1536]{1,0:T(1,128)}, bf16[256,1536]{1,0:T(8,128)(2,1)}) custom-call(bf16[256,1536]{1,0:T(8,128)(2,1)} %get-tuple-element.109.part, f32[64,1536]{1,0:T(8,128)} %get-tuple-element.85.base, f32[1,1536]{1,0:T(1,128)} %get-tuple-element.178.gain, f32[64,1536]{1,0:T(8,128)} %get-tuple-element.110.up), custom_call_target="tpu_custom_call" | custom-call | tf_op jit(solution)/shard_map/pallas_call | solution.py:352
  300.6 2.5 fusion.43.gm
  303.1 4.7 rec_back_first.1
  307.8 8.2 %shard_map.227.arriving = f32[8,512]{1,0:T(8,128)} custom-call(f32[8,512]{1,0:T(8,128)} %get-tuple-element.116.edge), custom_call_target="tpu_custom_call" | custom-call | tf_op jit(solution)/shard_map/pallas_call | solution.py:689
  316.0 5.6 %rec_back_second.1 = (bf16[256,512]{1,0:T(8,128)(2,1)}, bf16[256,512]{1,0:T(8,128)(2,1)}, f32[256,512]{1,0:T(8,128)}, f32[8,512]{1,0:T(8,128)}, f32[8,512]{1,0:T(8,128)}) custom-call(s32[1]{0:T(128)} %bitcast.22.core, f32[256,512]{1,0:T(8,128)} %get-tuple-element.114.beyond, f32[256,512]{1,0:T(8,128)} %get-tuple-element.115.local, ...), custom_call_target="tpu_custom_call" | custom-call | tf_op jit(solution)/shard_map/rec_back_second/pallas_call | solution.py:966
  322.5 1.4 collective-permute-start.13
  324.0 2.0 fusion.8
  327.2 6.6 %collective-permute-done.13 = f32[3,512]{1,0:T(4,128)S(1)} collective-permute-done((f32[3,512]{1,0:T(4,128)S(1)}, f32[3,512]{1,0:T(4,128)S(1)}, u32[]{:S(2)}, u32[]{:S(2)}) %collective-permute-start.13) | collective-permute-done | bytes 6176 | tf_op jit(solution)/shard_map/ppermute | solution.py:1001
  335.7 1.5 fusion.6.part
  338.9 7.3 %shard_map.228 = bf16[768,2560]{1,0:T(8,128)(2,1)} custom-call(s32[1]{0:T(128)} %bitcast.22.core, bf16[256,1536]{1,0:T(8,128)(2,1)} %get-tuple-element.122.refs_0_.refs_4_, bf16[256,1536]{1,0:T(8,128)(2,1)} %collective-permute-done.14.refs_1_.refs_5_, bf16[256,512]{1,0:T(8,128)(2,1)} %copy-done.11, bf16[256,512]{1,0:T(8,128)(2,1)} %copy-done.33, ...), custom_call_target="tpu_custom_call" | custom-call | tf_op jit(solution)/shard_map/pallas_call | solution.py:634
  350.2 25.4 %shard_map.229 = (f32[64,1536]{1,0:T(8,128)}, f32[1,1536]{1,0:T(1,128)}, bf16[256,1536]{1,0:T(8,128)(2,1)}) custom-call(bf16[256,1536]{1,0:T(8,128)(2,1)} %fusion.6.part, f32[64,1536]{1,0:T(8,128)} %get-tuple-element.190.base, f32[1,1536]{1,0:T(1,128)} %get-tuple-element.179.gain, f32[64,1536]{1,0:T(8,128)} %get-tuple-element.126.up), custom_call_target="tpu_custom_call" | custom-call | tf_op jit(solution)/shard_map/pallas_call | solution.py:352
  375.7 1.4 pad_maximum_fusion.5.gains
  377.1 12.0 %totals.1 = (f32[4,1536]{1,0:T(4,128)}, f32[8,512]{1,0:T(8,128)}, bf16[32,512]{1,0:T(8,128)(2,1)}) custom-call(f32[4,1536]{1,0:T(4,128)} %pad_maximum_fusion.5.gains, f32[8,512]{1,0:T(8,128)} %get-tuple-element.131.chan, bf16[4,32,512]{2,1,0:T(8,128)(2,1)} %bitcast.199), custom_call_target="tpu_custom_call" | custom-call | tf_op jit(solution)/shard_map/totals/pallas_call | solution.py:466
  391.0 1.4 slice_select_fusion
  392.4 2.6 broadcast_select_fusion
  395.1 1.3 bitcast_convert_fusion
  397.8 58.9 %reduce-scatter.8.cloned.1.call-done = bf16[192,2560]{1,0:T(8,128)(2,1)} async-done(((bf16[768,2560]{1,0:T(8,128)(2,1)}), bf16[192,2560]{1,0:T(8,128)(2,1)}) %reduce-scatter.8.cloned.1.call-update) | async-done | bytes 983056 | tf_op jit(solution)/shard_map/reduce_scatter | solution.py:1051
  457.9 1.5 reshape.194
  464.0 4.5 copy.70
  468.5 24.0 %shard_map.230 = (f32[64,1536]{1,0:T(8,128)}, bf16[256,1536]{1,0:T(8,128)(2,1)}) custom-call(bf16[256,1536]{1,0:T(8,128)(2,1)} %get-tuple-element.135.part, f32[64,1536]{1,0:T(8,128)} %get-tuple-element.97.base, f32[1,1536]{1,0:T(1,128)} %get-tuple-element.176.gain), custom_call_target="tpu_custom_call" | custom-call | tf_op jit(solution)/shard_map/pallas_call | solution.py:284
  492.6 1.8 copy.71
  494.3 2.1 copy.102
  (221 shorter events, 47.3 us)
Async XLA Ops:
  7.2 122.0 %copy-start = (bf16[384,1536]{1,0:T(8,128)(2,1)S(1)}, bf16[384,1536]{1,0:T(8,128)(2,1)}, u32[]{:S(2)}) copy-start(bf16[384,1536]{1,0:T(8,128)(2,1)} %param.22) | copy-start | bytes 3538948
  7.2 17.5 %copy-start.43 = (f32[1,2,1536]{2,1,0:T(2,128)S(1)}, f32[1,2,1536]{2,1,0:T(2,128)}, u32[]{:S(2)}) copy-start(f32[1,2,1536]{2,1,0:T(2,128)} %param.15) | copy-start | bytes 36868
  7.2 21.6 %copy-start.12 = (bf16[2,256,1536]{2,1,0:T(8,128)(2,1)S(1)}, bf16[2,256,1536]{2,1,0:T(8,128)(2,1)}, u32[]{:S(2)}) copy-start(bf16[2,256,1536]{2,1,0:T(8,128)(2,1)} %param.25) | copy-start | bytes 4718596
  7.2 385.2 %reduce-scatter.6.cloned.1.call-start = ((), (), s32[]{:S(2)}) async-start(), calls=%async_computation.4 | async-start | bytes 6881280 | tf_op jit(solution)/shard_map/reduce_scatter | solution.py:1051
  14.1 47.9 %collective-permute-start.3 = (bf16[2,1536,1152]{2,1,0:T(8,128)(2,1)}, bf16[2,1536,1152]{2,1,0:T(8,128)(2,1)}, u32[]{:S(2)}, u32[]{:S(2)}) collective-permute-start(bf16[2,1536,1152]{2,1,0:T(8,128)(2,1)} %bitcast.175.own_in), channel_id=1, source_target_pairs={{0,16},{16,0},{1,17},{17,1},{2,18},{18,2},{3,19},{19,3},{4,20},{20... | collective-permute-start | bytes 21233672 | tf_op jit(solution)/shard_map/ppermute | solution.py:1005
  14.6 23.1 %copy-start.40 = (s32[1,256]{1,0:T(1,128)}, s32[1,256]{1,0:T(1,128)S(1)}, u32[]{:S(2)}) copy-start(s32[1,256]{1,0:T(1,128)S(1)} %constant_dynamic-slice_fusion.4.refs_0_) | copy-start | bytes 3076
  14.6 22.3 %collective-permute-start.2 = (s32[256]{0:T(256)S(1)}, s32[256]{0:T(256)}, u32[]{:S(2)}, u32[]{:S(2)}) collective-permute-start(s32[256]{0:T(256)S(1)} %bitcast.201), channel_id=1, source_target_pairs={{0,4},{4,8},{8,12},{1,5},{5,9},{9,13},{2,6},{6,10},{10,14},{3,7},{... | collective-permute-start | bytes 3080 | tf_op jit(solution)/shard_map/ppermute | solution.py:1001
  21.1 18.6 %collective-permute-start = (bf16[16,1536]{1,0:T(8,128)(2,1)}, bf16[16,1536]{1,0:T(8,128)(2,1)}, u32[]{:S(2)}, u32[]{:S(2)}) collective-permute-start(bf16[16,1536]{1,0:T(8,128)(2,1)} %dynamic-slice_bitcast_fusion.3), channel_id=1, source_target_pairs={{0,4},{4,8},{8,12},{1,5},{5,9},{9,13},{2,6},{6,10},{10,14},{3,7},{... | collective-permute-start | bytes 147464 | tf_op jit(solution)/shard_map/ppermute | solution.py:1001
  24.7 13.2 %collective-permute-start.1 = (f32[2,1536]{1,0:T(2,128)S(1)}, f32[2,1536]{1,0:T(2,128)}, u32[]{:S(2)}, u32[]{:S(2)}) collective-permute-start(f32[2,1536]{1,0:T(2,128)S(1)} %bitcast.208), channel_id=1, source_target_pairs={{0,16},{16,0},{1,17},{17,1},{2,18},{18,2},{3,19},{19,3},{4,20},{20... | collective-permute-start | bytes 36872 | tf_op jit(solution)/shard_map/ppermute | solution.py:1005
  24.7 37.3 %collective-permute-start.4 = (bf16[1152,1536]{1,0:T(8,128)(2,1)}, bf16[1152,1536]{1,0:T(8,128)(2,1)}, u32[]{:S(2)}, u32[]{:S(2)}) collective-permute-start(bf16[1152,1536]{1,0:T(8,128)(2,1)} %bitcast.177), channel_id=1, source_target_pairs={{0,16},{16,0},{1,17},{17,1},{2,18},{18,2},{3,19},{19,3},{4,20},{20... | collective-permute-start | bytes 10616840 | tf_op jit(solution)/shard_map/ppermute | solution.py:1005
  50.4 10.6 %copy-start.41 = (s32[1,256]{1,0:T(1,128)S(1)}, s32[1,256]{1,0:T(1,128)}, u32[]{:S(2)}) copy-start(s32[1,256]{1,0:T(1,128)} %copy-done.40) | copy-start | bytes 3076
  50.4 10.7 %copy-start.47 = (pred[1024]{0:T(1024)(128)(4,1)S(1)}, pred[1024]{0:T(1024)(128)(4,1)}, u32[]{:S(2)}) copy-start(pred[1024]{0:T(1024)(128)(4,1)} %broadcast_compare_fusion) | copy-start | bytes 3076
  50.4 10.7 %copy-start.48 = (s32[256]{0:T(256)S(1)}, s32[256]{0:T(256)}, u32[]{:S(2)}) copy-start(s32[256]{0:T(256)} %iota_add_fusion.1) | copy-start | bytes 3076
  62.0 60.4 %copy-start.13 = (bf16[1536,384]{1,0:T(8,128)(2,1)S(1)}, bf16[1536,384]{1,0:T(8,128)(2,1)}, u32[]{:S(2)}) copy-start(bf16[1536,384]{1,0:T(8,128)(2,1)} %param.20) | copy-start | bytes 3538948
  164.2 4.3 collective-permute-start.5
  164.3 3.3 collective-permute-start.6
  164.7 3.7 collective-permute-start.7
  179.1 213.3 %reduce-scatter.4.cloned.1.call-start = ((), (), s32[]{:S(2)}) async-start(), calls=%async_computation.3 | async-start | bytes 6881280 | tf_op jit(solution)/shard_map/reduce_scatter | solution.py:1051
  180.0 80.1 %collective-permute-start.8 = (bf16[256,1536]{1,0:T(8,128)(2,1)}, bf16[256,1536]{1,0:T(8,128)(2,1)}, u32[]{:S(2)}, u32[]{:S(2)}) collective-permute-start(bf16[256,1536]{1,0:T(8,128)(2,1)} %get-tuple-element.102.refs_0_), channel_id=1, source_target_pairs={{0,16},{16,0},{1,17},{17,1},{2,18},{18,2},{3,19},{19,3},{4,20},{20... | collective-permute-start | bytes 2359304 | tf_op jit(solution)/shard_map/ppermute | solution.py:1005
  218.7 38.1 %copy-start.25 = (bf16[256,1152]{1,0:T(8,128)(2,1)S(1)}, bf16[256,1152]{1,0:T(8,128)(2,1)}, u32[]{:S(2)}) copy-start(bf16[256,1152]{1,0:T(8,128)(2,1)} %get-tuple-element.106.refs_6_) | copy-start | bytes 1769476
  256.7 4.3 collective-permute-start.10
  256.8 3.3 collective-permute-start.11
  257.3 3.7 collective-permute-start.9
  270.8 29.8 %copy-start.5 = (bf16[512,1536]{1,0:T(8,128)(2,1)S(1)}, bf16[512,1536]{1,0:T(8,128)(2,1)}, u32[]{:S(2)}) copy-start(bf16[512,1536]{1,0:T(8,128)(2,1)} %w_out.1) | copy-start | bytes 4718596
  270.8 186.0 %reduce-scatter.8.cloned.1.call-start = ((), (), s32[]{:S(2)}) async-start(), calls=%async_computation.5 | async-start | bytes 4915200 | tf_op jit(solution)/shard_map/reduce_scatter | solution.py:1051
  271.9 55.1 %collective-permute-start.14 = (bf16[256,1536]{1,0:T(8,128)(2,1)S(1)}, bf16[256,1536]{1,0:T(8,128)(2,1)}, u32[]{:S(2)}, u32[]{:S(2)}) collective-permute-start(bf16[256,1536]{1,0:T(8,128)(2,1)S(1)} %copy-done.9), channel_id=1, source_target_pairs={{0,16},{16,0},{1,17},{17,1},{2,18},{18,2},{3,19},{19,3},{4,20},{20... | collective-permute-start | bytes 2359304 | tf_op jit(solution)/shard_map/ppermute | solution.py:1005
  272.1 50.4 %collective-permute-start.18 = (bf16[256,512]{1,0:T(8,128)(2,1)}, bf16[256,512]{1,0:T(8,128)(2,1)}, u32[]{:S(2)}, u32[]{:S(2)}) collective-permute-start(bf16[256,512]{1,0:T(8,128)(2,1)} %get-tuple-element.123.refs_10_), channel_id=1, source_target_pairs={{0,16},{16,0},{1,17},{17,1},{2,18},{18,2},{3,19},{19,3},{4,20},{20... | collective-permute-start | bytes 786440 | tf_op jit(solution)/shard_map/ppermute | solution.py:1005
  273.3 61.9 %collective-permute-start.19 = (bf16[256,1536]{1,0:T(8,128)(2,1)S(1)}, bf16[256,1536]{1,0:T(8,128)(2,1)}, u32[]{:S(2)}, u32[]{:S(2)}) collective-permute-start(bf16[256,1536]{1,0:T(8,128)(2,1)S(1)} %copy-done.10), channel_id=1, source_target_pairs={{0,16},{16,0},{1,17},{17,1},{2,18},{18,2},{3,19},{19,3},{4,20},{20... | collective-permute-start | bytes 2359304 | tf_op jit(solution)/shard_map/ppermute | solution.py:1005
  274.3 62.9 %collective-permute-start.22 = (bf16[256,1536]{1,0:T(8,128)(2,1)}, bf16[256,1536]{1,0:T(8,128)(2,1)}, u32[]{:S(2)}, u32[]{:S(2)}) collective-permute-start(bf16[256,1536]{1,0:T(8,128)(2,1)} %get-tuple-element.98.refs_20_), channel_id=1, source_target_pairs={{0,16},{16,0},{1,17},{17,1},{2,18},{18,2},{3,19},{19,3},{4,20},{20... | collective-permute-start | bytes 2359304 | tf_op jit(solution)/shard_map/ppermute | solution.py:1005
  303.1 34.1 %collective-permute-start.17 = (bf16[256,1536]{1,0:T(8,128)(2,1)}, bf16[256,1536]{1,0:T(8,128)(2,1)S(1)}, u32[]{:S(2)}, u32[]{:S(2)}) collective-permute-start(bf16[256,1536]{1,0:T(8,128)(2,1)} %get-tuple-element.111.refs_8_), channel_id=1, source_target_pairs={{0,16},{16,0},{1,17},{17,1},{2,18},{18,2},{3,19},{19,3},{4,20},{20... | collective-permute-start | bytes 2359304 | tf_op jit(solution)/shard_map/ppermute | solution.py:1005
  307.8 16.1 %copy-start.15 = (bf16[256,512]{1,0:T(8,128)(2,1)S(1)}, bf16[256,512]{1,0:T(8,128)(2,1)}, u32[]{:S(2)}) copy-start(bf16[256,512]{1,0:T(8,128)(2,1)} %get-tuple-element.121.refs_6_) | copy-start | bytes 786436
  321.6 12.2 %copy-start.38 = (bf16[256,256]{1,0:T(8,128)(2,1)S(1)}, bf16[256,256]{1,0:T(8,128)(2,1)}, u32[]{:S(2)}) copy-start(bf16[256,256]{1,0:T(8,128)(2,1)} %get-tuple-element.124.refs_18_) | copy-start | bytes 393220
  321.6 12.9 %copy-start.18 = (bf16[256,384]{1,0:T(8,128)(2,1)S(1)}, bf16[256,384]{1,0:T(8,128)(2,1)}, u32[]{:S(2)}) copy-start(bf16[256,384]{1,0:T(8,128)(2,1)} %copy.61.refs_14_) | copy-start | bytes 589828
  321.6 14.0 %copy-start.4 = (bf16[1536,2,512]{2,0,1:T(8,128)(2,1)S(1)}, bf16[1536,2,512]{2,0,1:T(8,128)(2,1)}, u32[]{:S(2)}) copy-start(bf16[1536,2,512]{2,0,1:T(8,128)(2,1)} %copy.100) | copy-start | bytes 9437188
  322.5 11.3 %collective-permute-start.13 = (f32[3,512]{1,0:T(4,128)S(1)}, f32[3,512]{1,0:T(4,128)S(1)}, u32[]{:S(2)}, u32[]{:S(2)}) collective-permute-start(f32[3,512]{1,0:T(4,128)S(1)} %slice.102), channel_id=1, source_target_pairs={{4,0},{8,4},{12,8},{5,1},{9,5},{13,9},{6,2},{10,6},{14,10},{7,3},{... | collective-permute-start | bytes 18440 | tf_op jit(solution)/shard_map/ppermute | solution.py:1001
  327.1 7.5 %collective-permute-start.23 = (bf16[256,384]{1,0:T(8,128)(2,1)S(1)}, bf16[256,384]{1,0:T(8,128)(2,1)S(1)}, u32[]{:S(2)}, u32[]{:S(2)}) collective-permute-start(bf16[256,384]{1,0:T(8,128)(2,1)S(1)} %copy-done.17), channel_id=1, source_target_pairs={{0,16},{16,0},{1,17},{17,1},{2,18},{18,2},{3,19},{19,3},{4,20},{20... | collective-permute-start | bytes 589832 | tf_op jit(solution)/shard_map/ppermute | solution.py:1005
  333.8 1.5 collective-permute-start.21
  334.6 2.6 collective-permute-start.20
  335.2 2.1 collective-permute-start.16
  335.2 2.0 collective-permute-start.15
  347.2 1.5 collective-permute-start.24
  347.3 1.8 collective-permute-start.25
  347.9 27.8 %copy-start.44 = (f32[1,1536]{1,0:T(1,128)S(1)}, f32[1,1536]{1,0:T(1,128)}, u32[]{:S(2)}) copy-start(f32[1,1536]{1,0:T(1,128)} %get-tuple-element.130) | copy-start | bytes 18436
  347.9 27.8 %copy-start.45 = (f32[1,1536]{1,0:T(1,128)S(1)}, f32[1,1536]{1,0:T(1,128)}, u32[]{:S(2)}) copy-start(f32[1,1536]{1,0:T(1,128)} %get-tuple-element.129) | copy-start | bytes 18436
  347.9 27.8 %copy-start.46 = (f32[1,1536]{1,0:T(1,128)S(1)}, f32[1,1536]{1,0:T(1,128)}, u32[]{:S(2)}) copy-start(f32[1,1536]{1,0:T(1,128)} %get-tuple-element.128) | copy-start | bytes 18436
  375.7 19.4 %copy-start.22 = (bf16[256,1536]{1,0:T(8,128)(2,1)S(1)}, bf16[256,1536]{1,0:T(8,128)(2,1)}, u32[]{:S(2)}) copy-start(bf16[256,1536]{1,0:T(8,128)(2,1)} %get-tuple-element.137) | copy-start | bytes 2359300
  389.8 7.2 %collective-permute-start.26 = (bf16[16,512]{1,0:T(8,128)(2,1)S(1)}, bf16[16,512]{1,0:T(8,128)(2,1)S(1)}, u32[]{:S(2)}, u32[]{:S(2)}) collective-permute-start(bf16[16,512]{1,0:T(8,128)(2,1)S(1)} %dynamic-slice_bitcast_fusion.4), channel_id=1, source_target_pairs={{0,16},{16,0},{1,17},{17,1},{2,18},{18,2},{3,19},{19,3},{4,20},{20... | collective-permute-start | bytes 49160 | tf_op jit(solution)/shard_map/ppermute | solution.py:1005
  395.0 67.7 %collective-permute-start.12 = (bf16[384,1792]{1,0:T(8,128)(2,1)}, bf16[384,1792]{1,0:T(8,128)(2,1)S(1)}, u32[]{:S(2)}, u32[]{:S(2)}) collective-permute-start(bf16[384,1792]{1,0:T(8,128)(2,1)} %broadcast_select_fusion), channel_id=1, source_target_pairs={{0,16},{16,0},{1,17},{17,1},{2,18},{18,2},{3,19},{19,3},{4,20},{20... | collective-permute-start | bytes 4128776 | tf_op jit(solution)/shard_map/ppermute | solution.py:1005
  (34 other events, 75.3 us)
Sparse Core Ops, SparseCore 0:
  179.2 99.5 reduce-scatter.5
  281.1 99.7 reduce-scatter.3
  383.2 73.5 reduce-scatter.7
where the time goes:
time: 508 us; the launch traced here: 503 us
  Pallas kernels  307 us (60%)
  waiting for transfers between devices  73.7 us (15%)
  local copies, waits for them, and re-layouts  47.9 us (9%)
  other arithmetic  23.1 us (5%)
  matrix products  20.3 us (4%)
  starting transfers between devices  15.8 us (3%)
  between operations  14.9 us (3%)
    pallas_call x3, Pallas kernels, join_backward(): pl.pallas_call(functools.partial(backward_body, n), out_shape=(jax.ShapeD...  77.3 us
    pallas_call x2, Pallas kernels, join_mlp(): pl.pallas_call(functools.partial(body, n), out_shape=tuple(outs), in_spec...  61.5 us
    reduce_scatter x3, waiting for transfers between devices, seq_scatter(): return lax.psum_scatter(grad, 'seq', scatter_dimension=0, tiled=True)  58.9 us
    pallas_call x1, Pallas kernels, join_keys_back(): pl.pallas_call(functools.partial(keys_back_body, n, blocks, reach), name=...  38 us
    pallas_call x1, Pallas kernels, join_keys(): pl.pallas_call(functools.partial(keys_body, n, blocks, reach), name='join...  32.4 us
    unnamed x110, local copies, waits for them, and re-layouts  27.9 us
    pallas_call x3, Pallas kernels, weight_grad(): pl.pallas_call(functools.partial(weight_grad_body, sizes), grid_spec=pltp...  25 us
    pallas_call x1, Pallas kernels, join_forward(): pl.pallas_call(functools.partial(forward_body, n, kind), out_shape=(jax.S...  24 us
  transfers between devices with their start and end apart: 30, of which 8 were waited for; matrix products, arithmetic and copies ran while one was open for 12% of the time, Pallas kernels for 36%

commit v1 on v0

--- a/solution.py
+++ b/solution.py
@@ -98,12 +98,15 @@
         copy.wait()
 
 
-def forward_body(n, kind, part, base, gain, new, full, recv, s1, r1, s2, r2):
-    me = lax.axis_index("head")
+def own_part(array, me, rows):
+    core = lax.axis_index("section")
+    return array[core, pl.ds(pl.multiple_of(me * rows, rows), rows)].astype(F32)
+
+
+def forward_rows(n, me, kind, part, base, gain, new, full, recv, s1, r1, s2, r2):
     rows = base.shape[0]
-    meet("head", me, n)
     sent = scatter_start(n, me, rows, part, recv, s1, r1)
-    fresh = base[...] + scatter_sum(me, rows, part, recv, sent)
+    fresh = base + scatter_sum(me, rows, part, recv, sent)
     new[...] = fresh
     out = fresh
     if kind != "last":
@@ -113,25 +116,162 @@
     drain(sent)
 
 
-def forward_mlp_body(n, part, base, gain, own_in, own_out, other_in, other_out, *refs):
-    new, full, gate_up, hidden, part_next, recv, s1, r1, s2, r2, acc, b_in, b_out, sems = refs
+def forward_body(n, kind, part, base, gain, new, full, recv, s1, r1, s2, r2):
+    me = lax.axis_index("head")
+    meet("head", me, n)
+    forward_rows(n, me, kind, part, base[...], gain, new, full, recv, s1, r1, s2, r2)
+
+
+def meet_axes(axes):
+    barrier = pltpu.get_barrier_semaphore()
+    for axis, me, n in axes:
+        for k in range(1, n):
+            pl.semaphore_signal(
+                barrier, inc=1, device_id={axis: lax.rem(me + k, n)}, device_id_type=MESH
+            )
+    pl.semaphore_wait(barrier, sum(n - 1 for _, _, n in axes))
+
+
+def mixing_body(
+    n, blocks, edge, ids, local, through, gate_pre, w_out, inputs, gain, own_in, own_out, other_in, other_out,
+    entering, all_ids, state_out, mixed, new, full, gate_up, hidden, part_next,
+    every, c1, c2, c3, c4, part, recv, s1, r1, s2, r2, acc, b_in, b_out, sems,
+):
     own, other = (own_in, own_out), (other_in, other_out)
+    me, place = lax.axis_index("head"), lax.axis_index("seq")
+    rows = part.shape[0] // n
+    all_ids[place] = ids[...]
+    meet_axes((("head", me, n), ("seq", place, blocks)))
+    carried = carry_start(blocks, place, edge, every, c1, c2)
     fetch_weights(0, own, other, (b_in, b_out), sems)
-    forward_body(n, "keep", part, base, gain, new, full, recv, s1, r1, s2, r2)
+    id_copies = []
+    for k in range(1, blocks):
+        peer = lax.rem(place + k, blocks)
+        id_copies.append(
+            remote(ids, all_ids.at[place], c3.at[k - 1], c4.at[k - 1], "seq", peer)
+        )
+    for copy in id_copies:
+        copy.start()
+    act = gelu_parts(gate_pre[...])[0]
+    finish(carried)
+    state_in = carry_state(blocks, place, False, every, edge.shape[1])
+    entering[...] = jnp.broadcast_to(state_in, entering.shape)
+    state = local[...] + through[...] * state_in
+    state_out[...] = state
+    low = (state * act).astype(BF16)
+    mixed[...] = low
+    part[...] = jnp.dot(low, w_out[...], preferred_element_type=F32).astype(BF16)
+    base = own_part(inputs, me, rows)
+    forward_rows(n, me, "keep", part, base, gain, new, full, recv, s1, r1, s2, r2)
+    finish(id_copies)
     wait_weights(own, (b_in, b_out), sems)
     mlp_forward_part(full, (b_in, b_out), gate_up, hidden, part_next, acc)
 
 
-def forward_both_body(n, part, base, gain, low, own_in, own_out, other_in, other_out, *refs):
-    new, full, hidden, mine, theirs, part_last, part_back = refs[:7]
-    recv, s1, r1, s2, r2, acc, acc_back, b_in, b_out, sems = refs[7:]
+def mixing(edge, ids, local, through, gate_pre, w_out, inputs, gain, weights, ident):
+    n, blocks = lax.axis_size("head"), lax.axis_size("seq")
+    count, chans = local.shape
+    width = w_out.shape[1]
+    rows = count // n
+    units = weights[1].shape[0]
+    dma = pltpu.SemaphoreType.DMA
+    f32, wide = jax.ShapeDtypeStruct((count, chans), F32), jax.ShapeDtypeStruct((count, width), BF16)
+    outs = (
+        jax.ShapeDtypeStruct(edge.shape, F32),
+        jax.ShapeDtypeStruct((blocks,) + ids.shape, jnp.int32),
+        f32,
+        jax.ShapeDtypeStruct((count, chans), BF16),
+        jax.ShapeDtypeStruct((rows, width), F32),
+        wide,
+        jax.ShapeDtypeStruct((TILES, count, 2 * units // TILES), F32),
+        jax.ShapeDtypeStruct((count, units), BF16),
+        wide,
+    )
+    return pl.pallas_call(
+        functools.partial(mixing_body, n, blocks),
+        name="mixing",
+        out_shape=outs,
+        in_specs=[vmem()] * 8 + [pl.BlockSpec(memory_space=pl.ANY)] * 4,
+        out_specs=tuple(vmem() for _ in outs),
+        scratch_shapes=[pltpu.VMEM((blocks - 1,) + edge.shape, F32)]
+        + [dma((blocks - 1,))] * 4
+        + [pltpu.VMEM((count, width), BF16)]
+        + boundary_scratch(n, rows, width)
+        + mlp_scratch(count, width, units, 1),
+        compiler_params=pltpu.CompilerParams(collective_id=ident, has_side_effects=True),
+    )(edge, ids, local, through, gate_pre, w_out, inputs, gain, *weights)
+
+
+def last_layer_body(n, part, base, gain, top, own_in, own_out, other_in, other_out, *refs):
+    new, full, hidden, mine, part_last, part_back, full_other, hidden_other, mine_other = refs[:9]
+    recv, s1, r1, s2, r2, theirs, core_sem, acc, acc_back, b_in, b_out, sems = refs[9:]
     own, other = (own_in, own_out), (other_in, other_out)
+    me, core = lax.axis_index("head"), lax.axis_index("section")
+    tile = b_out.shape[1]
     fetch_weights(1, own, other, (b_in, b_out), sems)
-    forward_body(n, "keep", part, base, gain, new, full, recv, s1, r1, s2, r2)
+    meet_axes((("head", me, n), ("section", core, 2)))
+    forward_rows(n, me, "keep", part, base[...], gain, new, full, recv, s1, r1, s2, r2)
+
+    def to_other(src, dst, t, j):
+        return remote(src, dst, core_sem.at[0, j, t], core_sem.at[1, j, t], "section", 1 - core)
+
+    whole = to_other(full, full_other, 0, 2)
+    whole.start()
     wait_weights(own, (b_in, b_out), sems)
-    mlp_both_part(
-        full, low, (b_in, b_out), hidden, mine, theirs, part_last, part_back, acc, acc_back
-    )
+    acc[...] = jnp.zeros_like(acc)
+    acc_back[...] = jnp.zeros_like(acc_back)
+
+    def tile_copies(t):
+        at = tile_columns(t, tile)
+        return (
+            to_other(theirs.at[:, at], mine_other.at[:, at], t, 0),
+            to_other(hidden.at[:, at], hidden_other.at[:, at], t, 1),
+        )
+
+    @pl.loop(0, TILES)
+    def _(t):
+        both = jnp.dot(full[...], b_in[t], preferred_element_type=F32)
+        gate, up = both[:, :tile], both[:, tile:]
+        at = tile_columns(t, tile)
+        act = grad_tile(top[core], gate, up, b_in[t], b_out[t], mine, theirs, at, acc_back)
+        value = (act * up).astype(BF16)
+        hidden[:, at] = value
+        for copy in tile_copies(t):
+            copy.start()
+        acc[...] += jnp.dot(value, b_out[t], preferred_element_type=F32)
+
+    part_last[...] = acc[...].astype(BF16)
+    part_back[...] = acc_back[...].astype(BF16)
+    whole.wait()
+
+    @pl.loop(0, TILES)
+    def _(t):
+        for copy in tile_copies(t):
+            copy.wait()
+
+
+def last_layer(part, base, gain, top, weights, ident):
+    n = lax.axis_size("head")
+    count, width = part.shape
+    rows = base.shape[0]
+    units = weights[1].shape[0]
+    wide = jax.ShapeDtypeStruct((count, width), BF16)
+    narrow = jax.ShapeDtypeStruct((count, units), BF16)
+    outs = (
+        jax.ShapeDtypeStruct((rows, width), F32),
+        wide, narrow, narrow, wide, wide, wide, narrow, narrow,
+    )
+    return pl.pallas_call(
+        functools.partial(last_layer_body, n),
+        name="last_layer",
+        out_shape=outs,
+        in_specs=[vmem()] * 4 + [pl.BlockSpec(memory_space=pl.ANY)] * 4,
+        out_specs=tuple(vmem() for _ in outs),
+        scratch_shapes=boundary_scratch(n, rows, width)
+        + [pltpu.VMEM((count, units), BF16), pltpu.SemaphoreType.DMA((2, 3, TILES))]
+        + mlp_scratch(count, width, units, 2),
+        compiler_params=pltpu.CompilerParams(collective_id=ident, has_side_effects=True),
+    )(part, base, gain, top, *weights)
 
 
 def meet_around(n, me, blocks, place, pairs):
@@ -195,11 +335,13 @@
 
 def backward_body(n, part, base, gain, up, res, gain_grad, full, recv, s1, r1, s2, r2):
     me = lax.axis_index("head")
-    rows = base.shape[0]
+    rows = res.shape[0]
     meet("head", me, n)
     sent = scatter_start(n, me, rows, part, recv, s1, r1)
     grad = scatter_sum(me, rows, part, recv, sent)
-    out, gain_grad[...] = norm_back_rows(grad, base[...], gain[...], up[...])
+    v = own_part(base, me, rows) if len(base.shape) == 3 else base[...]
+    above = own_part(up, me, rows) if len(up.shape) == 3 else up[...]
+    out, gain_grad[...] = norm_back_rows(grad, v, gain[...], above)
     res[...] = out
     finish(spread(n, me, rows, out.astype(BF16), full, s2, r2))
     drain(sent)
@@ -294,31 +436,6 @@
     )(part, base, gain)
 
 
-def join_mlp(part, base, gain, weights, ident, low=None):
-    n = lax.axis_size("head")
-    count, width = part.shape
-    rows = base.shape[0]
-    units = weights[1].shape[0]
-    whole = jax.ShapeDtypeStruct((count, width), BF16)
-    narrow = jax.ShapeDtypeStruct((count, units), BF16)
-    outs = [jax.ShapeDtypeStruct((rows, width), F32), whole]
-    if low is None:
-        body, operands = forward_mlp_body, [part, base, gain]
-        outs += [jax.ShapeDtypeStruct((TILES, count, 2 * units // TILES), F32), narrow, whole]
-    else:
-        body, operands = forward_both_body, [part, base, gain, low]
-        outs += [narrow, narrow, narrow, whole, whole]
-    return pl.pallas_call(
-        functools.partial(body, n),
-        out_shape=tuple(outs),
-        in_specs=[vmem()] * len(operands) + [pl.BlockSpec(memory_space=pl.ANY)] * 4,
-        out_specs=tuple(vmem() for _ in outs),
-        scratch_shapes=boundary_scratch(n, rows, width)
-        + mlp_scratch(count, width, units, 1 if low is None else 2),
-        compiler_params=pltpu.CompilerParams(collective_id=ident, has_side_effects=True),
-    )(*operands, *weights)
-
-
 def join_keys(part, base, gain, w_kv, reach, ident):
     n, blocks = lax.axis_size("head"), lax.axis_size("seq")
     count, width = part.shape
@@ -348,7 +465,7 @@
 def join_backward(part, base, gain, up, ident):
     n = lax.axis_size("head")
     count, width = part.shape
-    rows = base.shape[0]
+    rows = count // n
     return pl.pallas_call(
         functools.partial(backward_body, n),
         out_shape=(
@@ -571,25 +688,6 @@
     part[...] = acc[...].astype(BF16)
 
 
-def mlp_both_part(x, low, buffers, hidden, mine, theirs, part, part_back, acc, acc_back):
-    tile = buffers[1].shape[1]
-    acc[...] = jnp.zeros_like(acc)
-    acc_back[...] = jnp.zeros_like(acc_back)
-
-    @pl.loop(0, TILES)
-    def _(t):
-        both = jnp.dot(x[...], buffers[0][t], preferred_element_type=F32)
-        gate, up = both[:, :tile], both[:, tile:]
-        at = tile_columns(t, tile)
-        act = grad_tile(low[...], gate, up, buffers[0][t], buffers[1][t], mine, theirs, at, acc_back)
-        value = (act * up).astype(BF16)
-        hidden[:, at] = value
-        acc[...] += jnp.dot(value, buffers[1][t], preferred_element_type=F32)
-
-    part[...] = acc[...].astype(BF16)
-    part_back[...] = acc_back[...].astype(BF16)
-
-
 def mlp_scratch(count, width, units, accs):
     tile = units // TILES
     return [pltpu.VMEM((count, width), F32)] * accs + [
@@ -611,8 +709,11 @@
             near, far = right[:, window], right_other[:, window]
         else:
             near, far = right[...], right_other[...]
-        total = lax.dot_general(left[...], near, over, preferred_element_type=F32)
-        total += lax.dot_general(left_other[...], far, over, preferred_element_type=F32)
+        left, left_other = (
+            ref[0] if len(ref.shape) == 3 else ref[...] for ref in (left, left_other)
+        )
+        total = lax.dot_general(left, near, over, preferred_element_type=F32)
+        total += lax.dot_general(left_other, far, over, preferred_element_type=F32)
         out[:, start : start + size] = total.astype(BF16)
         start += size
 
@@ -629,7 +730,14 @@
         else:
             rows = pl.BlockSpec((count, tile), lambda i, core: (0, i))
         full = pl.BlockSpec(right.shape, lambda i, core: (0, 0))
-        in_specs += [rows, rows, full, full]
+        if left.ndim == 3:
+            in_specs += [
+                pl.BlockSpec((1, count, tile), lambda i, core: (core[0], 0, i)),
+                pl.BlockSpec((1, count, tile), lambda i, core: (1 - core[0], 0, i)),
+            ]
+        else:
+            in_specs += [rows, rows]
+        in_specs += [full, full]
         operands += [left, left_other, right, right_other]
     return pl.pallas_call(
         functools.partial(weight_grad_body, sizes),
@@ -643,57 +751,46 @@
     )(core, *operands)
 
 
-def carry_body(n, reverse, edge, *refs):
-    me = lax.axis_index("seq")
-    if reverse:
-        out, every, send_sem, recv_sem = refs
-    else:
-        ids, out, all_ids, every, send_sem, recv_sem, send_ids, recv_ids = refs
-        all_ids[me] = ids[...]
-    meet("seq", me, n)
+def carry_start(n, me, edge, every, send_sem, recv_sem):
     copies = []
     for k in range(1, n):
         peer = lax.rem(me + k, n)
         copies.append(
             remote(edge, every.at[k - 1], send_sem.at[k - 1], recv_sem.at[k - 1], "seq", peer)
         )
-        if not reverse:
-            copies.append(
-                remote(ids, all_ids.at[me], send_ids.at[k - 1], recv_ids.at[k - 1], "seq", peer)
-            )
     for copy in copies:
         copy.start()
-    finish(copies)
-    state = jnp.zeros((1, edge.shape[1]), F32)
-    order = range(1, n) if reverse else range(n - 1, 0, -1)
-    for k in order:
-        sender = me - k if not reverse else me + n - k
-        inside = sender >= 0 if not reverse else sender < n
-        if reverse:
-            inside = jnp.logical_and(inside, sender > me)
+    return copies
+
+
+def carry_state(n, me, reverse, every, width):
+    state = jnp.zeros((1, width), F32)
+    for k in range(1, n) if reverse else range(n - 1, 0, -1):
+        inside = me + n - k < n if reverse else me - k >= 0
         slot = every[k - 1]
         state = jnp.where(inside, slot[0:1] * state + slot[1:2], state)
-    out[...] = jnp.broadcast_to(state, out.shape)
-
-
-def carry(edge, ident, ids=None):
+    return state
+
+
+def carry_body(n, edge, out, every, send_sem, recv_sem):
+    me = lax.axis_index("seq")
+    meet("seq", me, n)
+    finish(carry_start(n, me, edge, every, send_sem, recv_sem))
+    out[...] = jnp.broadcast_to(carry_state(n, me, True, every, edge.shape[1]), out.shape)
+
+
+def carry_back(edge, ident):
     n = lax.axis_size("seq")
     dma = pltpu.SemaphoreType.DMA((n - 1,))
-    scratch = [pltpu.VMEM((n - 1,) + edge.shape, F32), dma, dma]
-    shapes = [jax.ShapeDtypeStruct(edge.shape, F32)]
-    operands = [edge]
-    if ids is not None:
-        scratch += [dma, dma]
-        shapes.append(jax.ShapeDtypeStruct((n,) + ids.shape, jnp.int32))
-        operands.append(ids)
     return pl.pallas_call(
-        functools.partial(carry_body, n, ids is None),
-        out_shape=tuple(shapes),
-        in_specs=[vmem() for _ in operands],
-        out_specs=tuple(vmem() for _ in shapes),
-        scratch_shapes=scratch,
+        functools.partial(carry_body, n),
+        name="carry_back",
+        out_shape=jax.ShapeDtypeStruct(edge.shape, F32),
+        in_specs=[vmem()],
+        out_specs=vmem(),
+        scratch_shapes=[pltpu.VMEM((n - 1,) + edge.shape, F32), dma, dma],
         compiler_params=pltpu.CompilerParams(collective_id=ident, has_side_effects=True),
-    )(*operands)
+    )(edge)
 
 
 def shifted(x, by, row, fill):
@@ -732,19 +829,34 @@
     return (pltpu.roll(ids, k, 0)[16:] == ids[16:]).astype(F32)
 
 
+def soft_plus(x):
+    e = jnp.exp(-jnp.abs(x))
+    series = jnp.full_like(e, 1.0 / 8.0)
+    for k in range(7, 0, -1):
+        series = 1.0 / k - e * series
+    return jnp.maximum(x, 0.0) + jnp.where(e < 0.05, e * series, jnp.log(1.0 + e))
+
+
+def id_columns(row):
+    return jnp.broadcast_to(row.astype(F32), (128, row.shape[1])).T
+
+
 def rec_forward_body(
-    x, gain, w_in, ids, chan, soft, gates,
-    normed, gate_pre, ext, conv_out, pre_out, through, local, edge, low_x,
+    spot, x, before, gain, w_in, segments, before_ids, chan, gates,
+    normed, ids, gate_pre, ext, conv_out, pre_out, through, local, edge, low_x,
 ):
     count, block = conv_out.shape
 
     @pl.when(pl.program_id(0) == 0)
     def _():
-        v = x[...].astype(F32)
-        out = v * lax.rsqrt(jnp.mean(v * v, axis=-1, keepdims=True) + EPSILON) * gain[...]
-        low = out.astype(BF16)
-        low_x[...] = low
-        normed[...] = low[16:]
+        for v, at in ((before[0], slice(0, 16)), (x[0], slice(16, count + 16))):
+            v = v.astype(F32)
+            out = v * lax.rsqrt(jnp.mean(v * v, axis=-1, keepdims=True) + EPSILON) * gain[...]
+            low_x[at] = out.astype(BF16)
+        normed[...] = low_x[16:]
+        earlier = id_columns(before_ids[pl.ds(spot[0], 1)])[count - 16 :]
+        ids[0:16] = jnp.where(spot[1] == 0, -1.0, earlier)
+        ids[16:] = id_columns(segments[pl.ds(spot[0], 1)])
 
     values = jnp.dot(low_x[...], w_in[0], preferred_element_type=F32).astype(BF16)
     gate_pre[...] = jnp.dot(low_x[16:], w_in[1], preferred_element_type=F32)
@@ -760,7 +872,7 @@
     gate = pre[:, block:] + chan[6:7]
     pre_out[0] = rate
     pre_out[1] = gate
-    log_decay = -8.0 * jax.nn.sigmoid(rate) * soft[...]
+    log_decay = -8.0 * jax.nn.sigmoid(rate) * soft_plus(chan[7:8])
     decay = jnp.exp(log_decay) * same_rows(ids[...], 1)
     drive = jnp.sqrt(minus_expm1(2.0 * log_decay)) * jax.nn.sigmoid(gate) * low.astype(F32)
     row = lax.broadcasted_iota(jnp.int32, (count, block), 0)
@@ -772,20 +884,47 @@
     edge[2:8] = jnp.zeros((6, block), F32)
 
 
-def rec_forward(x, gain, w_in, ids, chan, soft, gates):
-    count, width = x.shape[0] - 16, x.shape[1]
+def rec_forward(spot, inputs, before, gain, w_in, segments, before_ids, chan, gates):
+    _, count, width = inputs.shape
     chans = w_in.shape[2]
     blocks, block = gates.shape[:2]
-    wide = pl.BlockSpec((count, block), lambda i: (0, i))
-    row8 = pl.BlockSpec((8, block), lambda i: (0, i))
-    tall = pl.BlockSpec((count + 16, block), lambda i: (0, i))
+    wide = pl.BlockSpec((count, block), lambda i, spot: (0, i))
+    row8 = pl.BlockSpec((8, block), lambda i, spot: (0, i))
+    tall = pl.BlockSpec((count + 16, block), lambda i, spot: (0, i))
+    flat = pl.BlockSpec(segments.shape, lambda i, spot: (0, 0))
     f32 = jax.ShapeDtypeStruct((count, chans), F32)
     return pl.pallas_call(
         rec_forward_body,
         name="rec_forward",
-        grid=(blocks,),
+        grid_spec=pltpu.PrefetchScalarGridSpec(
+            num_scalar_prefetch=1,
+            grid=(blocks,),
+            in_specs=[
+                pl.BlockSpec((1, count, width), lambda i, spot: (spot[0], 0, 0)),
+                pl.BlockSpec((1, 16, width), lambda i, spot: (spot[0], 0, 0)),
+                pl.BlockSpec((1, width), lambda i, spot: (0, 0)),
+                pl.BlockSpec((2, width, block), lambda i, spot: (0, 0, i)),
+                flat,
+                flat,
+                row8,
+                pl.BlockSpec((1, block, 2 * block), lambda i, spot: (i, 0, 0)),
+            ],
+            out_specs=(
+                pl.BlockSpec((count, width), lambda i, spot: (0, 0)),
+                pl.BlockSpec((count + 16, 128), lambda i, spot: (0, 0)),
+                wide,
+                tall,
+                wide,
+                pl.BlockSpec((2, count, block), lambda i, spot: (0, 0, i)),
+                wide,
+                wide,
+                row8,
+            ),
+            scratch_shapes=[pltpu.VMEM((count + 16, width), BF16)],
+        ),
         out_shape=(
             jax.ShapeDtypeStruct((count, width), BF16),
+            jax.ShapeDtypeStruct((count + 16, 128), F32),
             f32,
             jax.ShapeDtypeStruct((count + 16, chans), BF16),
             jax.ShapeDtypeStruct((count, chans), BF16),
@@ -794,79 +933,15 @@
             f32,
             jax.ShapeDtypeStruct((8, chans), F32),
         ),
-        in_specs=[
-            pl.BlockSpec((count + 16, width), lambda i: (0, 0)),
-            pl.BlockSpec((1, width), lambda i: (0, 0)),
-            pl.BlockSpec((2, width, block), lambda i: (0, 0, i)),
-            pl.BlockSpec((count + 16, 128), lambda i: (0, 0)),
-            row8,
-            pl.BlockSpec((1, block), lambda i: (0, i)),
-            pl.BlockSpec((1, block, 2 * block), lambda i: (i, 0, 0)),
-        ],
-        out_specs=(
-            pl.BlockSpec((count, width), lambda i: (0, 0)),
-            wide,
-            tall,
-            wide,
-            pl.BlockSpec((2, count, block), lambda i: (0, 0, i)),
-            wide,
-            wide,
-            row8,
-        ),
-        scratch_shapes=[pltpu.VMEM((count + 16, width), BF16)],
-    )(x, gain, w_in, ids, chan, soft, gates)
-
-
-def rec_finish_body(steps, local, through, entering, gate_pre, w_out, hidden, mixed, part, acc):
-    step = pl.program_id(0)
-
-    @pl.when(step == 0)
-    def _():
-        acc[...] = jnp.zeros_like(acc)
-
-    state = local[...] + through[...] * entering[0:1]
-    hidden[...] = state
-    low = (state * gelu_parts(gate_pre[...])[0]).astype(BF16)
-    mixed[...] = low
-    acc[...] += jnp.dot(low, w_out[...], preferred_element_type=F32)
-
-    @pl.when(step == steps - 1)
-    def _():
-        part[...] = acc[...].astype(BF16)
-
-
-def rec_finish(local, through, entering, gate_pre, w_out):
-    count, chans = local.shape
-    width = w_out.shape[1]
-    tile = chans // 2
-    wide = pl.BlockSpec((count, tile), lambda i: (0, i))
-    return pl.pallas_call(
-        functools.partial(rec_finish_body, 2),
-        name="rec_finish",
-        grid=(2,),
-        out_shape=(
-            jax.ShapeDtypeStruct((count, chans), F32),
-            jax.ShapeDtypeStruct((count, chans), BF16),
-            jax.ShapeDtypeStruct((count, width), BF16),
-        ),
-        in_specs=[
-            wide,
-            wide,
-            pl.BlockSpec((8, tile), lambda i: (0, i)),
-            wide,
-            pl.BlockSpec((tile, width), lambda i: (i, 0)),
-        ],
-        out_specs=(wide, wide, pl.BlockSpec((count, width), lambda i: (0, 0))),
-        scratch_shapes=[pltpu.VMEM((count, width), F32)],
-    )(local, through, entering, gate_pre, w_out)
-
-
-def rec_back_first_body(gm, gate_pre, hidden, rate, soft, ids, grad_gate, beyond, local, edge):
+    )(spot, inputs, before, gain, w_in, segments, before_ids, chan, gates)
+
+
+def rec_back_first_body(gm, gate_pre, hidden, rate, chan, ids, grad_gate, beyond, local, edge):
     count, block = gm.shape
     act, slope = gelu_parts(gate_pre[...])
     up = gm[...]
     grad_gate[...] = (up * hidden[...] * slope).astype(BF16)
-    decay = jnp.exp(-8.0 * jax.nn.sigmoid(rate[0]) * soft[...]) * same_rows(ids[...], 1)
+    decay = jnp.exp(-8.0 * jax.nn.sigmoid(rate[0]) * soft_plus(chan[7:8])) * same_rows(ids[...], 1)
     row = lax.broadcasted_iota(jnp.int32, (count, block), 0)
     a, b = scan_rows(shifted(decay, -1, row, 1.0), up * act, row, -1)
     beyond[...] = a
@@ -876,7 +951,7 @@
     edge[2:8] = jnp.zeros((6, block), F32)
 
 
-def rec_back_first(gm, gate_pre, hidden, pre, soft, ids, block):
+def rec_back_first(gm, gate_pre, hidden, pre, chan, ids, block):
     count, chans = gm.shape
     wide = pl.BlockSpec((count, block), lambda i: (0, i))
     row8 = pl.BlockSpec((8, block), lambda i: (0, i))
@@ -895,15 +970,15 @@
             wide,
             wide,
             pl.BlockSpec((1, count, block), lambda i: (0, 0, i)),
-            pl.BlockSpec((1, block), lambda i: (0, i)),
+            row8,
             pl.BlockSpec((count + 16, 128), lambda i: (0, 0)),
         ],
         out_specs=(wide, wide, wide, row8),
-    )(gm, gate_pre, hidden, pre, soft, ids)
+    )(gm, gate_pre, hidden, pre, chan, ids)
 
 
 def rec_back_second_body(
-    core, beyond, local, arriving, hidden, entering, pre, conv, chan, soft, gates, ids, ext,
+    core, beyond, local, arriving, hidden, entering, pre, conv, chan, gates, ids, ext,
     mine, theirs, grad_values, edge, chan_grad,
 ):
     count, block = local.shape
@@ -911,14 +986,15 @@
     state = local[...] + beyond[...] * arriving[0:1]
     earlier = jnp.where(row >= 1, pltpu.roll(hidden[...], 1, 0), entering[0:1])
     low = conv[...].astype(F32)
+    soft = soft_plus(chan[7:8])
     keep_rate = jax.nn.sigmoid(pre[0])
-    log_decay = -8.0 * keep_rate * soft[...]
+    log_decay = -8.0 * keep_rate * soft
     decay = jnp.exp(log_decay)
     size = jnp.sqrt(minus_expm1(2.0 * log_decay))
     gate = jax.nn.sigmoid(pre[1])
     grad_decay = state * earlier * same_rows(ids[...], 1)
     grad_log = grad_decay * decay - state * gate * low * (decay * decay / size)
-    grad_rate = grad_log * (-8.0 * soft[...]) * keep_rate * (1.0 - keep_rate)
+    grad_rate = grad_log * (-8.0 * soft) * keep_rate * (1.0 - keep_rate)
     grad_gate = state * size * low * gate * (1.0 - gate)
     rate_low = grad_rate.astype(BF16)
     gate_low_part = grad_gate.astype(BF16)
@@ -956,7 +1032,7 @@
     )
 
 
-def rec_back_second(core, beyond, local, arriving, hidden, entering, pre, conv, chan, soft, gates, ids, ext):
+def rec_back_second(core, beyond, local, arriving, hidden, entering, pre, conv, chan, gates, ids, ext):
     count, chans = local.shape
     blocks, block = gates.shape[:2]
     wide = pl.BlockSpec((count, block), lambda i, core: (0, i))
@@ -978,7 +1054,6 @@
                 pair,
                 wide,
                 row8,
-                pl.BlockSpec((1, block), lambda i, core: (0, i)),
                 pl.BlockSpec((1, block, 2 * block), lambda i, core: (i, 0, 0)),
                 pl.BlockSpec((count + 16, 128), lambda i, core: (0, 0)),
                 pl.BlockSpec((count + 16, block), lambda i, core: (0, i)),
@@ -992,7 +1067,7 @@
             jax.ShapeDtypeStruct((8, chans), F32),
             jax.ShapeDtypeStruct((8, chans), F32),
         ),
-    )(core, beyond, local, arriving, hidden, entering, pre, conv, chan, soft, gates, ids, ext)
+    )(core, beyond, local, arriving, hidden, entering, pre, conv, chan, gates, ids, ext)
 
 
 def from_behind(array, axis, by):
@@ -1069,27 +1144,20 @@
     core = lax.axis_index("section")
     first = core == 0
     place = lax.axis_index("seq")
-    rank = lax.axis_index("head")
-    heads = lax.axis_size("head")
     blocks_seq = lax.axis_size("seq")
     _, count, width = inputs.shape
-    rows = count // heads
     chans = rec_in.shape[2]
     blocks, block = rec_gates.shape[:2]
 
     def pick(array, index):
         return lax.dynamic_index_in_dim(array, index, 0, keepdims=False)
 
-    def own_rows(array):
-        return lax.dynamic_slice_in_dim(array, rank * rows, rows, axis=0)
-
     core_ref = core[None].astype(jnp.int32)
+    spot = jnp.stack([core, place]).astype(jnp.int32)
+    before = from_behind(inputs[:, -16:], "seq", 1)
+    before_ids = from_behind(segments, "seq", 1)
     ids = pick(segments, core)
-    stream_low = pick(inputs, core)
-    top_low = pick(cotangent, core)
-    before = from_behind(stream_low[-16:], "seq", 1)
     reach = min(max(1, WINDOW // count), blocks_seq - 1)
-    before_ids = from_behind(ids, "seq", 1)
 
     own_in = jnp.swapaxes(mlp_in[0], 0, 1)
     own_out = mlp_out[0]
@@ -1102,24 +1170,12 @@
     weights = (own_in, own_out, other_in, other_out)
     rec_in_wide = jnp.swapaxes(rec_in, 0, 1)
 
-    before_ids = jnp.where(place == 0, -1, before_ids[-16:])
-    ext_ids = jnp.broadcast_to(jnp.concatenate([before_ids, ids])[:, None], (count + 16, 128))
-    soft = jax.nn.softplus(rec_chan[7:8])
     gates_flat = rec_gates.reshape(blocks, block, 2 * block)
-    normed_one, gate_pre, ext, conv_low, pre, through, local, edge = rec_forward(
-        jnp.concatenate([before, stream_low]),
-        gain[0][0],
-        rec_in_wide,
-        ext_ids,
-        rec_chan,
-        soft,
-        gates_flat,
-    )
-    entering, every_id = carry(edge, 0, ids[None])
-    hidden_state, mixed, part = rec_finish(local, through, entering, gate_pre, rec_out)
-    stream_rows = own_rows(stream_low).astype(F32)
-    res_one, normed_a, gate_up_a, hidden_a, part = join_mlp(
-        part, stream_rows, gain[0][1], weights, 1
+    normed_one, ext_ids, gate_pre, ext, conv_low, pre, through, local, edge = rec_forward(
+        spot, inputs, before, gain[0][0], rec_in_wide, segments, before_ids, rec_chan, gates_flat
+    )
+    entering, every_id, hidden_state, mixed, res_one, normed_a, gate_up_a, hidden_a, part = mixing(
+        edge, segments, local, through, gate_pre, rec_out, inputs, gain[0][1], weights, 1
     )
     passed, normed_two, all_keys = join_keys(part, res_one, gain[1][0], attn_kv, reach, 2)
 
@@ -1128,7 +1184,7 @@
     queries = dot(normed_two, attn_q, (1, 0), BF16).reshape(count, heads_here, head_dim)
     key_ids = jnp.concatenate(
         [
-            pick(every_id, lax.rem(place - distance + blocks_seq, blocks_seq))[0]
+            pick(pick(every_id, lax.rem(place - distance + blocks_seq, blocks_seq)), core)
             for distance in range(reach, 0, -1)
         ]
         + [ids]
@@ -1141,9 +1197,10 @@
     attended, log_totals = attend(queries, all_keys, allowed)
     attended = attended.reshape(count, heads_here * head_dim)
     part = dot(attended, attn_out, (1, 0), BF16)
-    res_two, normed_b, hidden_b, mine_b, theirs_b, part_last, part_b = join_mlp(
-        part, passed, gain[1][1], weights, 3, top_low
-    )
+    (
+        res_two, normed_b, hidden_b, mine_b, part_last, part_b, normed_b_other, hidden_b_other,
+        mine_b_other,
+    ) = last_layer(part, passed, gain[1][1], cotangent, weights, 3)
 
     units = hidden_b.shape[1]
     window = (units // 2 + 127) // 128 * 128
@@ -1154,11 +1211,14 @@
             (out_low, out_other, hidden, swapped(hidden), window),
         ]
 
-    terms = mlp_term(mine_b, theirs_b, normed_b, hidden_b, top_low, pick(cotangent, 1 - core))
+    terms = [
+        (normed_b, normed_b_other, mine_b, mine_b_other, units),
+        (cotangent, cotangent, hidden_b, hidden_b_other, window),
+    ]
     part, sum_b = lax.optimization_barrier((part_b, weight_grad(core_ref, terms, False)))
     sum_b = seq_scatter(sum_b)
     grad_res_two, gain_b, low_two = join_backward(
-        part, res_two, gain[1][1], own_rows(top_low).astype(F32), 5
+        part, res_two, gain[1][1], cotangent, 5
     )
 
     grad_att = dot(low_two, attn_out, (1, 1), BF16)
@@ -1193,12 +1253,12 @@
 
     grad_mixed = dot(mix_low, rec_out, (1, 1))
     grad_branch, beyond, local_grad, edge = rec_back_first(
-        grad_mixed, gate_pre, hidden_state, pre, soft, ext_ids, block
-    )
-    (arriving,) = carry(edge, 9)
+        grad_mixed, gate_pre, hidden_state, pre, rec_chan, ext_ids, block
+    )
+    arriving = carry_back(edge, 9)
     gate_mine, gate_theirs, grad_values, over_edge, chan_grad = rec_back_second(
         core_ref, beyond, local_grad, arriving, hidden_state, entering, pre, conv_low, rec_chan,
-        soft, gates_flat, ext_ids, ext,
+        gates_flat, ext_ids, ext,
     )
     from_next = from_behind(over_edge[:3], "seq", -1)
     grad_values = jnp.concatenate([grad_values[:-3], grad_values[-3:] + from_next]).astype(BF16)
@@ -1218,7 +1278,7 @@
     )
     part, rec_sum = lax.optimization_barrier((part, rec_sum))
     rec_sum = seq_scatter(rec_sum)
-    _, gain_one, grad_inputs = join_backward(part, stream_rows, gain[0][0], grad_res_one, 8)
+    _, gain_one, grad_inputs = join_backward(part, inputs, gain[0][0], grad_res_one, 8)
 
     def gate_grad(left, right):
         return jnp.einsum(

time: 508 us -> 496 us (0.976)
  waiting for transfers between devices: 73.7 us -> 65.3 us
  Pallas kernels: 307 us -> 315 us
  other arithmetic: 23.1 us -> 16.9 us
    pallas_call x1, Pallas kernels: 38 us -> 43.1 us  [join_keys_back(): pl.pallas_call(functools.partial(keys_back_body, n, blocks, reach), name=...]
    pallas_call x6 -> x4, Pallas kernels: 88.4 us -> 91.1 us  [the longest x1 38 us: mixing(): pl.pallas_call(functools.partial(mixing_body, n, blocks), name='mixing',...]
    unnamed x110 -> x98, local copies, waits for them, and re-layouts: 27.9 us -> 29.3 us
  transfers between devices with their start and end apart: 30 -> 27, of which waited for: 8 -> 8; matrix products, arithmetic and copies ran while one was open for 12% -> 10% of each run, Pallas kernels for 36% -> 36%
where the time goes in v1:
time: 496 us; the launch traced here: 492 us
  Pallas kernels  315 us (64%)
  waiting for transfers between devices  65.3 us (13%)
  local copies, waits for them, and re-layouts  46.3 us (9%)
  matrix products  19.4 us (4%)
  other arithmetic  16.9 us (3%)
  between operations  14.9 us (3%)
  starting transfers between devices  14.5 us (3%)
    pallas_call x3, Pallas kernels, join_backward(): pl.pallas_call(functools.partial(backward_body, n), out_shape=(jax.ShapeD...  78.4 us
    reduce_scatter x3, waiting for transfers between devices, seq_scatter(): return lax.psum_scatter(grad, 'seq', scatter_dimension=0, tiled=True)  56.2 us
    pallas_call x1, Pallas kernels, join_keys_back(): pl.pallas_call(functools.partial(keys_back_body, n, blocks, reach), name=...  43.1 us
    pallas_call x1, Pallas kernels, mixing(): pl.pallas_call(functools.partial(mixing_body, n, blocks), name='mixing',...  38 us
    pallas_call x1, Pallas kernels, last_layer(): pl.pallas_call(functools.partial(last_layer_body, n), name='last_layer',...  34.3 us
    pallas_call x1, Pallas kernels, join_keys(): pl.pallas_call(functools.partial(keys_body, n, blocks, reach), name='join...  30.7 us
    unnamed x98, local copies, waits for them, and re-layouts  29.3 us
    pallas_call x3, Pallas kernels, weight_grad(): pl.pallas_call(functools.partial(weight_grad_body, sizes), grid_spec=pltp...  25.2 us
  transfers between devices with their start and end apart: 27, of which 8 were waited for; matrix products, arithmetic and copies ran while one was open for 10% of the time, Pallas kernels for 36%

profile of v1, /device:TPU:0, one launch (start us, length us, event | category | flops | bytes accessed | tf_op | source)
XLA Modules:
  0.0 492.4 jit_solution(2711221632232975134)
XLA Ops:
  7.3 6.8 %copy.99 = bf16[1,1536,2,1152]{3,1,2,0:T(8,128)(2,1)} copy(bf16[1,1536,2,1152]{3,2,1,0:T(2,128)(2,1)} %param.23) | data formatting | bytes 14155776 | tf_op args[10]
  15.5 4.9 %collective-permute-start = (bf16[2,16,1536]{2,1,0:T(8,128)(2,1)S(1)}, bf16[2,16,1536]{2,1,0:T(8,128)(2,1)S(1)}, u32[]{:S(2)}, u32[]{:S(2)}) collective-permute-start(bf16[2,16,1536]{2,1,0:T(8,128)(2,1)S(1)} %slice.77), channel_id=1, source_target_pairs={{0,4},{4,8},{8,12},{1,5},{5,9},{9,13},{2,6},{6,10},{10,14},{3,7},{... | collective-permute-start | bytes 294920 | tf_op jit(solution)/shard_map/ppermute | solution.py:1076
  20.5 3.5 collective-permute-start.2
  24.7 4.1 copy.100
  29.7 1.2 collective-permute-done.1
  32.8 8.8 %rec_forward.1 = (bf16[256,1536]{1,0:T(8,128)(2,1)}, f32[272,128]{1,0:T(8,128)}, f32[256,512]{1,0:T(8,128)}, bf16[272,512]{1,0:T(8,128)(2,1)}, bf16[256,512]{1,0...) custom-call(s32[2]{0:T(128)} %pad_add_fusion.1.spot, ...), custom_call_target="tpu_custom_call" | custom-call | tf_op jit(solution)/shard_map/rec_forward/pallas_call | solution.py:896
  41.6 38.0 %mixing.1 = (f32[8,512]{1,0:T(8,128)}, s32[4,2,256]{2,1,0:T(2,128)}, f32[256,512]{1,0:T(8,128)}, bf16[256,512]{1,0:T(8,128)(2,1)}, f32[64,1536]{1,0:T(8,128)}, /...) custom-call(f32[8,512]{1,0:T(8,128)} %get-tuple-element.80.edge, ...), custom_call_target="tpu_custom_call" | custom-call | tf_op jit(solution)/shard_map/mixing/pallas_call | solution.py:190
  79.6 30.7 %join_keys.1 = (f32[64,1536]{1,0:T(8,128)}, bf16[256,1536]{1,0:T(8,128)(2,1)}, bf16[1024,256]{1,0:T(8,128)(2,1)}) custom-call(bf16[256,1536]{1,0:T(8,128)(2,1)} %get-tuple-element.84.part, f32[64,1536]{1,0:T(8,128)} %get-tuple-element.85.base, f32[1,1536]{1,0:T(1,128)} %get-tuple-element.179.gain, bf16[1536,256]{1,0:T(8,128)(2,1)} %w_kv.3), custom_call_target="tpu_custom_call" | custom-call | tf_op jit(solution)/shard_map/join_keys/pallas_call | solution.py:445
  110.3 1.8 convolution_convert_fusion.3
  115.3 1.1 fusion.14
  117.1 1.5 convolution_convert_fusion.1.part
  118.6 34.3 %last_layer.1 = (f32[64,1536]{1,0:T(8,128)}, bf16[256,1536]{1,0:T(8,128)(2,1)}, bf16[256,1152]{1,0:T(8,128)(2,1)}, bf16[256,1152]{1,0:T(8,128)(2,1)}, bf16[256,1...) custom-call(bf16[256,1536]{1,0:T(8,128)(2,1)} %convolution_convert_f, ...), custom_call_target="tpu_custom_call" | custom-call | tf_op jit(solution)/shard_map/last_layer/pallas_call | solution.py:264
  153.0 9.0 %shard_map.220 = bf16[1536,1792]{1,0:T(8,128)(2,1)} custom-call(s32[1]{0:T(128)} %bitcast.core, bf16[256,1536]{1,0:T(8,128)(2,1)} %get-tuple-element.92.refs_0_, bf16[256,1536]{1,0:T(8,128)(2,1)} %get-tuple-element.93.refs_1_, bf16[256,1152]{1,0:T(8,128)(2,1)} %get-tuple-element.94.refs_2_, bf16[256,1152]{1,0:T(8,128)(2,1)} %get-tuple-element.95.refs_3_, ...), custom_call_target="tpu_custom_call" | custom-call | tf_op jit(solution)/shard_map/pallas_call | solution.py:742
  162.0 27.0 %shard_map.221 = (f32[64,1536]{1,0:T(8,128)}, f32[1,1536]{1,0:T(1,128)}, bf16[256,1536]{1,0:T(8,128)(2,1)}) custom-call(bf16[256,1536]{1,0:T(8,128)(2,1)} %get-tuple-element.98.part, f32[64,1536]{1,0:T(8,128)} %get-tuple-element.99.base, f32[1,1536]{1,0:T(1,128)} %get-tuple-element.178.gain, bf16[2,256,1536]{2,1,0:T(8,128)(2,1)} %up.1), custom_call_target="tpu_custom_call" | custom-call | tf_op jit(solution)/shard_map/pallas_call | solution.py:469
  189.0 1.8 convolution_convert_fusion.2
  191.0 1.8 fusion.22
  192.8 3.1 fusion.2
  195.9 0.9 fusion.4
  200.0 1.5 convolution_convert_fusion.part
  201.5 43.1 %join_keys_back.1 = (f32[64,1536]{1,0:T(8,128)}, f32[1,1536]{1,0:T(1,128)}, bf16[256,1536]{1,0:T(8,128)(2,1)}, bf16[256,256]{1,0:T(8,128)(2,1)}, bf16[256,1152]{...) custom-call(bf16[256,1536]{1,0:T(8,128)(2,1)} %convolution_convert_fusion.part, ...), custom_call_target="tpu_custom_call" | custom-call | tf_op jit(solution)/shard_map/join_keys_back/pallas_call | solution.py:490
  245.3 2.7 collective-permute-done.6.refs_3_
  250.0 8.8 %shard_map.222 = bf16[1536,1792]{1,0:T(8,128)(2,1)} custom-call(s32[1]{0:T(128)} %bitcast.core, bf16[256,1536]{1,0:T(8,128)(2,1)} %get-tuple-element.104.refs_0_, bf16[256,1536]{1,0:T(8,128)(2,1)} %collective-permute-done.5.refs_1_, bf16[256,1152]{1,0:T(8,128)(2,1)} %get-tuple-element.105.refs_2_, bf16[256,1152]{1,0:T(8,128)(2,1)} %copy-done.23, ...), custom_call_target="tpu_custom_call" | custom-call | tf_op jit(solution)/shard_map/pallas_call | solution.py:742
  258.9 1.0 copy-done.9
  262.8 25.2 %shard_map.223 = (f32[64,1536]{1,0:T(8,128)}, f32[1,1536]{1,0:T(1,128)}, bf16[256,1536]{1,0:T(8,128)(2,1)}) custom-call(bf16[256,1536]{1,0:T(8,128)(2,1)} %get-tuple-element.111.part, f32[64,1536]{1,0:T(8,128)} %get-tuple-element.85.base, f32[1,1536]{1,0:T(1,128)} %get-tuple-element.180.gain, f32[64,1536]{1,0:T(8,128)} %get-tuple-element.112.up), custom_call_target="tpu_custom_call" | custom-call | tf_op jit(solution)/shard_map/pallas_call | solution.py:469
  288.0 2.5 fusion.42.gm
  290.5 4.7 rec_back_first.1
  295.3 10.0 %carry_back.1.arriving = f32[8,512]{1,0:T(8,128)} custom-call(f32[8,512]{1,0:T(8,128)} %get-tuple-element.119.edge), custom_call_target="tpu_custom_call" | custom-call | tf_op jit(solution)/shard_map/carry_back/pallas_call | solution.py:785
  305.3 5.6 %rec_back_second.1 = (bf16[256,512]{1,0:T(8,128)(2,1)}, bf16[256,512]{1,0:T(8,128)(2,1)}, f32[256,512]{1,0:T(8,128)}, f32[8,512]{1,0:T(8,128)}, f32[8,512]{1,0:T(8,128)}) custom-call(s32[1]{0:T(128)} %bitcast.core, f32[256,512]{1,0:T(8,128)} %get-tuple-element.117.beyond, f32[256,512]{1,0:T(8,128)} %get-tuple-element.118.local, ...), custom_call_target="tpu_custom_call" | custom-call | tf_op jit(solution)/shard_map/rec_back_second/pallas_call | solution.py:1042
  311.8 1.4 collective-permute-start.10
  313.2 2.0 fusion.8
  315.3 1.1 slice.146
  316.8 2.9 collective-permute-done.10
  322.7 1.5 fusion.6.part
  325.9 7.4 %shard_map.224 = bf16[768,2560]{1,0:T(8,128)(2,1)} custom-call(s32[1]{0:T(128)} %bitcast.core, bf16[256,1536]{1,0:T(8,128)(2,1)} %get-tuple-element.126.refs_0_.refs_4_, bf16[256,1536]{1,0:T(8,128)(2,1)} %collective-permute-done.11.refs_1_.refs_5_, bf16[256,512]{1,0:T(8,128)(2,1)} %copy-done.12, bf16[256,512]{1,0:T(8,128)(2,1)} %copy-done.29, ...), custom_call_target="tpu_custom_call" | custom-call | tf_op jit(solution)/shard_map/pallas_call | solution.py:742
  337.3 26.3 %shard_map.225 = (f32[64,1536]{1,0:T(8,128)}, f32[1,1536]{1,0:T(1,128)}, bf16[256,1536]{1,0:T(8,128)(2,1)}) custom-call(bf16[256,1536]{1,0:T(8,128)(2,1)} %fusion.6.part, bf16[2,256,1536]{2,1,0:T(8,128)(2,1)} %base.1, f32[1,1536]{1,0:T(1,128)} %get-tuple-element.181.gain, f32[64,1536]{1,0:T(8,128)} %get-tuple-element.130.up), custom_call_target="tpu_custom_call" | custom-call | tf_op jit(solution)/shard_map/pallas_call | solution.py:469
  363.6 1.4 pad_maximum_fusion.4.gains
  365.0 12.2 %totals.1 = (f32[4,1536]{1,0:T(4,128)}, f32[8,512]{1,0:T(8,128)}, bf16[32,512]{1,0:T(8,128)(2,1)}) custom-call(f32[4,1536]{1,0:T(4,128)} %pad_maximum_fusion.4.gains, f32[8,512]{1,0:T(8,128)} %get-tuple-element.135.chan, bf16[4,32,512]{2,1,0:T(8,128)(2,1)} %bitcast.182), custom_call_target="tpu_custom_call" | custom-call | tf_op jit(solution)/shard_map/totals/pallas_call | solution.py:583
  379.1 1.4 slice_select_fusion
  380.5 2.6 broadcast_select_fusion
  383.2 1.3 bitcast_convert_fusion
  386.0 56.2 %reduce-scatter.8.cloned.1.call-done = bf16[192,2560]{1,0:T(8,128)(2,1)} async-done(((bf16[768,2560]{1,0:T(8,128)(2,1)}), bf16[192,2560]{1,0:T(8,128)(2,1)}) %reduce-scatter.8.cloned.1.call-update) | async-done | bytes 983056 | tf_op jit(solution)/shard_map/reduce_scatter | solution.py:1126
  442.2 1.2 slice.111
  443.3 1.5 reshape.189
  449.0 2.0 pad_maximum_fusion
  451.1 24.1 %shard_map.226 = (f32[64,1536]{1,0:T(8,128)}, bf16[256,1536]{1,0:T(8,128)(2,1)}) custom-call(bf16[256,1536]{1,0:T(8,128)(2,1)} %get-tuple-element.139.part, f32[64,1536]{1,0:T(8,128)} %get-tuple-element.99.base, f32[1,1536]{1,0:T(1,128)} %get-tuple-element.178.gain), custom_call_target="tpu_custom_call" | custom-call | tf_op jit(solution)/shard_map/pallas_call | solution.py:426
  475.3 6.6 %copy.70 = f32[1,384,2,1152]{3,2,1,0:T(2,128)} copy(f32[1,384,2,1152]{3,1,2,0:T(8,128)} %bitcast.167) | data formatting | bytes 7077888
  481.9 1.7 copy.71
  483.6 2.1 copy.102
  (194 shorter events, 35.2 us)
Async XLA Ops:
  7.2 109.9 %copy-start = (bf16[384,1536]{1,0:T(8,128)(2,1)S(1)}, bf16[384,1536]{1,0:T(8,128)(2,1)}, u32[]{:S(2)}) copy-start(bf16[384,1536]{1,0:T(8,128)(2,1)} %param.22) | copy-start | bytes 3538948
  7.2 13.2 %copy-start.38 = (f32[1,2,1536]{2,1,0:T(2,128)S(1)}, f32[1,2,1536]{2,1,0:T(2,128)}, u32[]{:S(2)}) copy-start(f32[1,2,1536]{2,1,0:T(2,128)} %param.15) | copy-start | bytes 36868
  7.2 13.3 %copy-start.37 = (s32[2,256]{1,0:T(2,128)S(1)}, s32[2,256]{1,0:T(2,128)}, u32[]{:S(2)}) copy-start(s32[2,256]{1,0:T(2,128)} %ids.1) | copy-start | bytes 6148
  7.2 373.3 %reduce-scatter.6.cloned.1.call-start = ((), (), s32[]{:S(2)}) async-start(), calls=%async_computation.4 | async-start | bytes 6881280 | tf_op jit(solution)/shard_map/reduce_scatter | solution.py:1126
  14.1 27.5 %collective-permute-start.3 = (bf16[2,1536,1152]{2,1,0:T(8,128)(2,1)}, bf16[2,1536,1152]{2,1,0:T(8,128)(2,1)}, u32[]{:S(2)}, u32[]{:S(2)}) collective-permute-start(bf16[2,1536,1152]{2,1,0:T(8,128)(2,1)} %bitcast.162.own_in), channel_id=1, source_target_pairs={{0,16},{16,0},{1,17},{17,1},{2,18},{18,2},{3,19},{19,3},{4,20},{20... | collective-permute-start | bytes 21233672 | tf_op jit(solution)/shard_map/ppermute | solution.py:1080
  14.6 27.0 %collective-permute-start.4 = (bf16[1152,1536]{1,0:T(8,128)(2,1)}, bf16[1152,1536]{1,0:T(8,128)(2,1)}, u32[]{:S(2)}, u32[]{:S(2)}) collective-permute-start(bf16[1152,1536]{1,0:T(8,128)(2,1)} %bitcast.6.own_out), channel_id=1, source_target_pairs={{0,16},{16,0},{1,17},{17,1},{2,18},{18,2},{3,19},{19,3},{4,20},{20... | collective-permute-start | bytes 10616840 | tf_op jit(solution)/shard_map/ppermute | solution.py:1080
  15.5 16.6 %collective-permute-start = (bf16[2,16,1536]{2,1,0:T(8,128)(2,1)S(1)}, bf16[2,16,1536]{2,1,0:T(8,128)(2,1)S(1)}, u32[]{:S(2)}, u32[]{:S(2)}) collective-permute-start(bf16[2,16,1536]{2,1,0:T(8,128)(2,1)S(1)} %slice.77), channel_id=1, source_target_pairs={{0,4},{4,8},{8,12},{1,5},{5,9},{9,13},{2,6},{6,10},{10,14},{3,7},{... | collective-permute-start | bytes 294920 | tf_op jit(solution)/shard_map/ppermute | solution.py:1076
  20.4 10.4 %collective-permute-start.1 = (f32[2,1536]{1,0:T(2,128)S(1)}, f32[2,1536]{1,0:T(2,128)S(1)}, u32[]{:S(2)}, u32[]{:S(2)}) collective-permute-start(f32[2,1536]{1,0:T(2,128)S(1)} %bitcast.189), channel_id=1, source_target_pairs={{0,16},{16,0},{1,17},{17,1},{2,18},{18,2},{3,19},{19,3},{4,20},{20... | collective-permute-start | bytes 36872 | tf_op jit(solution)/shard_map/ppermute | solution.py:1080
  20.5 11.6 %collective-permute-start.2 = (s32[2,256]{1,0:T(2,128)S(1)}, s32[2,256]{1,0:T(2,128)S(1)}, u32[]{:S(2)}, u32[]{:S(2)}) collective-permute-start(s32[2,256]{1,0:T(2,128)S(1)} %copy-done.37), channel_id=1, source_target_pairs={{0,4},{4,8},{8,12},{1,5},{5,9},{9,13},{2,6},{6,10},{10,14},{3,7},{... | collective-permute-start | bytes 6152 | tf_op jit(solution)/shard_map/ppermute | solution.py:1076
  24.0 88.9 %copy-start.36 = (s32[1,256]{1,0:T(1,128)}, s32[1,256]{1,0:T(1,128)S(1)}, u32[]{:S(2)}) copy-start(s32[1,256]{1,0:T(1,128)S(1)} %constant_dynamic-slice_fusion.3) | copy-start | bytes 3076
  24.1 88.9 %copy-start.42 = (s32[256]{0:T(256)}, s32[256]{0:T(256)S(1)}, u32[]{:S(2)}) copy-start(s32[256]{0:T(256)S(1)} %iota_add_fusion.1) | copy-start | bytes 3076
  24.1 88.9 %copy-start.43 = (pred[1024]{0:T(1024)(128)(4,1)}, pred[1024]{0:T(1024)(128)(4,1)S(1)}, u32[]{:S(2)}) copy-start(pred[1024]{0:T(1024)(128)(4,1)S(1)} %broadcast_compare_fusion) | copy-start | bytes 3076
  41.6 68.7 %copy-start.13 = (bf16[1536,384]{1,0:T(8,128)(2,1)S(1)}, bf16[1536,384]{1,0:T(8,128)(2,1)}, u32[]{:S(2)}) copy-start(bf16[1536,384]{1,0:T(8,128)(2,1)} %param.20) | copy-start | bytes 3538948
  161.9 218.6 %reduce-scatter.4.cloned.1.call-start = ((), (), s32[]{:S(2)}) async-start(), calls=%async_computation.3 | async-start | bytes 6881280 | tf_op jit(solution)/shard_map/reduce_scatter | solution.py:1126
  190.9 58.1 %collective-permute-start.5 = (bf16[256,1536]{1,0:T(8,128)(2,1)}, bf16[256,1536]{1,0:T(8,128)(2,1)}, u32[]{:S(2)}, u32[]{:S(2)}) collective-permute-start(bf16[256,1536]{1,0:T(8,128)(2,1)} %get-tuple-element.104.refs_0_), channel_id=1, source_target_pairs={{0,16},{16,0},{1,17},{17,1},{2,18},{18,2},{3,19},{19,3},{4,20},{20... | collective-permute-start | bytes 2359304 | tf_op jit(solution)/shard_map/ppermute | solution.py:1080
  201.5 43.7 %copy-start.22 = (bf16[256,1152]{1,0:T(8,128)(2,1)S(1)}, bf16[256,1152]{1,0:T(8,128)(2,1)}, u32[]{:S(2)}) copy-start(bf16[256,1152]{1,0:T(8,128)(2,1)} %get-tuple-element.108.refs_6_) | copy-start | bytes 1769476
  244.7 4.3 collective-permute-start.7
  244.7 3.3 collective-permute-start.6
  245.2 3.7 collective-permute-start.8
  258.8 29.2 %copy-start.5 = (bf16[512,1536]{1,0:T(8,128)(2,1)S(1)}, bf16[512,1536]{1,0:T(8,128)(2,1)}, u32[]{:S(2)}) copy-start(bf16[512,1536]{1,0:T(8,128)(2,1)} %w_out.1) | copy-start | bytes 4718596
  258.8 183.3 %reduce-scatter.8.cloned.1.call-start = ((), (), s32[]{:S(2)}) async-start(), calls=%async_computation.5 | async-start | bytes 4915200 | tf_op jit(solution)/shard_map/reduce_scatter | solution.py:1126
  259.9 51.9 %collective-permute-start.11 = (bf16[256,1536]{1,0:T(8,128)(2,1)S(1)}, bf16[256,1536]{1,0:T(8,128)(2,1)}, u32[]{:S(2)}, u32[]{:S(2)}) collective-permute-start(bf16[256,1536]{1,0:T(8,128)(2,1)S(1)} %copy-done.9), channel_id=1, source_target_pairs={{0,16},{16,0},{1,17},{17,1},{2,18},{18,2},{3,19},{19,3},{4,20},{20... | collective-permute-start | bytes 2359304 | tf_op jit(solution)/shard_map/ppermute | solution.py:1080
  260.1 64.1 %collective-permute-start.16 = (bf16[256,1536]{1,0:T(8,128)(2,1)S(1)}, bf16[256,1536]{1,0:T(8,128)(2,1)}, u32[]{:S(2)}, u32[]{:S(2)}) collective-permute-start(bf16[256,1536]{1,0:T(8,128)(2,1)S(1)} %copy-done.10), channel_id=1, source_target_pairs={{0,16},{16,0},{1,17},{17,1},{2,18},{18,2},{3,19},{19,3},{4,20},{20... | collective-permute-start | bytes 2359304 | tf_op jit(solution)/shard_map/ppermute | solution.py:1080
  261.2 63.0 %collective-permute-start.19 = (bf16[256,1536]{1,0:T(8,128)(2,1)}, bf16[256,1536]{1,0:T(8,128)(2,1)}, u32[]{:S(2)}, u32[]{:S(2)}) collective-permute-start(bf16[256,1536]{1,0:T(8,128)(2,1)} %get-tuple-element.100.refs_20_), channel_id=1, source_target_pairs={{0,16},{16,0},{1,17},{17,1},{2,18},{18,2},{3,19},{19,3},{4,20},{20... | collective-permute-start | bytes 2359304 | tf_op jit(solution)/shard_map/ppermute | solution.py:1080
  262.3 54.1 %collective-permute-start.17 = (bf16[256,384]{1,0:T(8,128)(2,1)}, bf16[256,384]{1,0:T(8,128)(2,1)}, u32[]{:S(2)}, u32[]{:S(2)}) collective-permute-start(bf16[256,384]{1,0:T(8,128)(2,1)} %copy.61.refs_14_), channel_id=1, source_target_pairs={{0,16},{16,0},{1,17},{17,1},{2,18},{18,2},{3,19},{19,3},{4,20},{20... | collective-permute-start | bytes 589832 | tf_op jit(solution)/shard_map/ppermute | solution.py:1080
  262.6 49.2 %collective-permute-start.18 = (bf16[256,256]{1,0:T(8,128)(2,1)}, bf16[256,256]{1,0:T(8,128)(2,1)S(1)}, u32[]{:S(2)}, u32[]{:S(2)}) collective-permute-start(bf16[256,256]{1,0:T(8,128)(2,1)} %get-tuple-element.128.refs_18_), channel_id=1, source_target_pairs={{0,16},{16,0},{1,17},{17,1},{2,18},{18,2},{3,19},{19,3},{4,20},{20... | collective-permute-start | bytes 393224 | tf_op jit(solution)/shard_map/ppermute | solution.py:1080
  290.5 21.3 %copy-start.11 = (bf16[256,1536]{1,0:T(8,128)(2,1)S(1)}, bf16[256,1536]{1,0:T(8,128)(2,1)}, u32[]{:S(2)}) copy-start(bf16[256,1536]{1,0:T(8,128)(2,1)} %get-tuple-element.113.refs_8_) | copy-start | bytes 2359300
  295.3 18.0 %copy-start.14 = (bf16[256,512]{1,0:T(8,128)(2,1)S(1)}, bf16[256,512]{1,0:T(8,128)(2,1)}, u32[]{:S(2)}) copy-start(bf16[256,512]{1,0:T(8,128)(2,1)} %get-tuple-element.125.refs_6_) | copy-start | bytes 786436
  310.9 5.5 %copy-start.26 = (bf16[256,512]{1,0:T(8,128)(2,1)S(1)}, bf16[256,512]{1,0:T(8,128)(2,1)}, u32[]{:S(2)}) copy-start(bf16[256,512]{1,0:T(8,128)(2,1)} %get-tuple-element.127.refs_10_) | copy-start | bytes 786436
  310.9 8.8 %copy-start.16 = (bf16[256,384]{1,0:T(8,128)(2,1)S(1)}, bf16[256,384]{1,0:T(8,128)(2,1)}, u32[]{:S(2)}) copy-start(bf16[256,384]{1,0:T(8,128)(2,1)} %copy.62.refs_22_) | copy-start | bytes 589828
  310.9 11.8 %copy-start.4 = (bf16[1536,2,512]{2,0,1:T(8,128)(2,1)S(1)}, bf16[1536,2,512]{2,0,1:T(8,128)(2,1)}, u32[]{:S(2)}) copy-start(bf16[1536,2,512]{2,0,1:T(8,128)(2,1)} %copy.100) | copy-start | bytes 9437188
  311.8 12.5 %collective-permute-start.14 = (bf16[256,1536]{1,0:T(8,128)(2,1)S(1)}, bf16[256,1536]{1,0:T(8,128)(2,1)S(1)}, u32[]{:S(2)}, u32[]{:S(2)}) collective-permute-start(bf16[256,1536]{1,0:T(8,128)(2,1)S(1)} %copy-done.11), channel_id=1, source_target_pairs={{0,16},{16,0},{1,17},{17,1},{2,18},{18,2},{3,19},{19,3},{4,20},{20... | collective-permute-start | bytes 2359304 | tf_op jit(solution)/shard_map/ppermute | solution.py:1080
  311.8 12.4 %copy-start.33 = (bf16[256,256]{1,0:T(8,128)(2,1)}, bf16[256,256]{1,0:T(8,128)(2,1)S(1)}, u32[]{:S(2)}) copy-start(bf16[256,256]{1,0:T(8,128)(2,1)S(1)} %collective-permute-done.18.refs_19_) | copy-start | bytes 393220
  311.8 7.8 %collective-permute-start.10 = (f32[3,512]{1,0:T(4,128)S(1)}, f32[3,512]{1,0:T(4,128)S(1)}, u32[]{:S(2)}, u32[]{:S(2)}) collective-permute-start(f32[3,512]{1,0:T(4,128)S(1)} %slice.90), channel_id=1, source_target_pairs={{4,0},{8,4},{12,8},{5,1},{9,5},{13,9},{6,2},{10,6},{14,10},{7,3},{... | collective-permute-start | bytes 18440 | tf_op jit(solution)/shard_map/ppermute | solution.py:1076
  316.4 4.9 %collective-permute-start.15 = (bf16[256,512]{1,0:T(8,128)(2,1)S(1)}, bf16[256,512]{1,0:T(8,128)(2,1)S(1)}, u32[]{:S(2)}, u32[]{:S(2)}) collective-permute-start(bf16[256,512]{1,0:T(8,128)(2,1)S(1)} %copy-done.26), channel_id=1, source_target_pairs={{0,16},{16,0},{1,17},{17,1},{2,18},{18,2},{3,19},{19,3},{4,20},{20... | collective-permute-start | bytes 786440 | tf_op jit(solution)/shard_map/ppermute | solution.py:1080
  319.6 1.4 collective-permute-start.20
  321.1 3.1 collective-permute-start.13
  322.5 1.8 collective-permute-start.12
  334.3 1.5 collective-permute-start.21
  334.6 1.6 collective-permute-start.22
  334.9 28.6 %copy-start.39 = (f32[1,1536]{1,0:T(1,128)S(1)}, f32[1,1536]{1,0:T(1,128)}, u32[]{:S(2)}) copy-start(f32[1,1536]{1,0:T(1,128)} %get-tuple-element.134) | copy-start | bytes 18436
  335.0 28.6 %copy-start.40 = (f32[1,1536]{1,0:T(1,128)S(1)}, f32[1,1536]{1,0:T(1,128)}, u32[]{:S(2)}) copy-start(f32[1,1536]{1,0:T(1,128)} %get-tuple-element.133) | copy-start | bytes 18436
  335.0 28.6 %copy-start.41 = (f32[1,1536]{1,0:T(1,128)S(1)}, f32[1,1536]{1,0:T(1,128)}, u32[]{:S(2)}) copy-start(f32[1,1536]{1,0:T(1,128)} %get-tuple-element.132) | copy-start | bytes 18436
  363.6 19.7 %copy-start.20 = (bf16[256,1536]{1,0:T(8,128)(2,1)S(1)}, bf16[256,1536]{1,0:T(8,128)(2,1)}, u32[]{:S(2)}) copy-start(bf16[256,1536]{1,0:T(8,128)(2,1)} %get-tuple-element.141) | copy-start | bytes 2359300
  378.7 6.5 %collective-permute-start.23 = (bf16[16,512]{1,0:T(8,128)(2,1)S(1)}, bf16[16,512]{1,0:T(8,128)(2,1)S(1)}, u32[]{:S(2)}, u32[]{:S(2)}) collective-permute-start(bf16[16,512]{1,0:T(8,128)(2,1)S(1)} %dynamic-slice_bitcast_fusion), channel_id=1, source_target_pairs={{0,16},{16,0},{1,17},{17,1},{2,18},{18,2},{3,19},{19,3},{4,20},{20... | collective-permute-start | bytes 49160 | tf_op jit(solution)/shard_map/ppermute | solution.py:1080
  380.5 4.7 copy-start.35
  383.1 64.9 %collective-permute-start.9 = (bf16[384,1792]{1,0:T(8,128)(2,1)}, bf16[384,1792]{1,0:T(8,128)(2,1)S(1)}, u32[]{:S(2)}, u32[]{:S(2)}) collective-permute-start(bf16[384,1792]{1,0:T(8,128)(2,1)} %broadcast_select_fusion), channel_id=1, source_target_pairs={{0,16},{16,0},{1,17},{17,1},{2,18},{18,2},{3,19},{19,3},{4,20},{20... | collective-permute-start | bytes 4128776 | tf_op jit(solution)/shard_map/ppermute | solution.py:1080
  475.3 10.4 %copy-start.1 = (bf16[384,1536]{1,0:T(8,128)(2,1)S(1)}, bf16[384,1536]{1,0:T(8,128)(2,1)}, u32[]{:S(2)}) copy-start(bf16[384,1536]{1,0:T(8,128)(2,1)} %param.22) | copy-start | bytes 3538948
  (25 other events, 42.5 us)
Sparse Core Ops, SparseCore 0:
  162.1 102.5 reduce-scatter.5
  267.0 99.6 reduce-scatter.3
  369.0 73.1 reduce-scatter.7
